TPU v7x, 128 devices: a whole 4x4x4 slice. The times are simulated.
128 devices in a mesh: part: 1, data: 16 (over z, y), stage: 8 (over x, core).
Axes of the slice: x: 4, y: 4, z: 4, core: 2. Of those that a mesh axis runs over, the one named last changes fastest.
Arguments:
- x_in: bfloat16 [32, 128, 1536], P(('part', 'data'))
- y_tgt: bfloat16 [32, 128, 1536], P(('part', 'data'))
- w_up: bfloat16 [8, 1536, 6144], P('stage')
- w_down: bfloat16 [8, 6144, 1536], P('stage')
- gain: float32 [8, 1536], P('stage')
Outputs:
- output 1: float32 [8, 1536, 6144], P(('part', 'stage'))
- output 2: float32 [8, 6144, 1536], P(('part', 'stage'))
- output 3: float32 [8, 1536], P(('part', 'stage'))
- output 4: float32 [1], P('part')
All inputs are finite; a program needn't handle non-finite values.
Results may differ from a plain program's by a relative error of at most 0.00377391.
Values are sent between devices in bfloat16 or wider.
A program may use at most 1 GiB of HBM per device.

v0:
```python
import jax
import jax.numpy as jnp
from jax import lax
from jax.sharding import PartitionSpec as P

EPS = 1e-6
ROW_DIMS = (((0,), (0,)), ((), ()))
LAST_DIMS = (((1,), (1,)), ((), ()))


def layer_fwd(x_rows, w_one, w_two, gain_row):
    x_float = x_rows.astype(jnp.float32)
    inv_rms = lax.rsqrt(jnp.mean(x_float * x_float, axis=-1, keepdims=True) + EPS)
    normed = (x_float * inv_rms * gain_row).astype(jnp.bfloat16)
    pre_act = jnp.dot(normed, w_one, preferred_element_type=jnp.float32)
    hidden = jax.nn.gelu(pre_act).astype(jnp.bfloat16)
    update = jnp.dot(hidden, w_two, preferred_element_type=jnp.float32)
    return (x_float + update).astype(jnp.bfloat16)


def layer_bwd(x_rows, d_out, w_one, w_two, gain_row):
    x_float = x_rows.astype(jnp.float32)
    inv_rms = lax.rsqrt(jnp.mean(x_float * x_float, axis=-1, keepdims=True) + EPS)
    unit_x = x_float * inv_rms
    normed = (unit_x * gain_row).astype(jnp.bfloat16)
    pre_act = jnp.dot(normed, w_one, preferred_element_type=jnp.float32)
    act_full, gelu_back = jax.vjp(jax.nn.gelu, pre_act)
    hidden = act_full.astype(jnp.bfloat16)
    g_two = lax.dot_general(hidden, d_out, ROW_DIMS, preferred_element_type=jnp.float32)
    d_hidden = lax.dot_general(d_out, w_two, LAST_DIMS, preferred_element_type=jnp.float32)
    d_pre = gelu_back(d_hidden)[0].astype(jnp.bfloat16)
    g_one = lax.dot_general(normed, d_pre, ROW_DIMS, preferred_element_type=jnp.float32)
    d_normed = lax.dot_general(d_pre, w_one, LAST_DIMS, preferred_element_type=jnp.float32)
    g_gain = jnp.sum(d_normed * unit_x, axis=0)
    d_unit = d_normed * gain_row
    d_x = inv_rms * (d_unit - unit_x * jnp.mean(d_unit * unit_x, axis=-1, keepdims=True))
    return (d_out.astype(jnp.float32) + d_x).astype(jnp.bfloat16), g_one, g_two, g_gain


def stage_fwd(x_rows, old_saved, w_one, w_two, gains):
    layer_inputs = []
    hidden_x = x_rows
    for layer_id in range(w_one.shape[0]):
        layer_inputs.append(hidden_x)
        hidden_x = layer_fwd(hidden_x, w_one[layer_id], w_two[layer_id], gains[layer_id])
    return hidden_x, jnp.stack(layer_inputs)


def keep_fwd(x_rows, old_saved, w_one, w_two, gains):
    return x_rows, old_saved


def stage_bwd(saved_x, d_out, w_one, w_two, gains, acc_all):
    list_one = []
    list_two = []
    list_gain = []
    d_rows = d_out
    for layer_id in reversed(range(w_one.shape[0])):
        d_rows, g_one, g_two, g_gain = layer_bwd(saved_x[layer_id], d_rows, w_one[layer_id], w_two[layer_id], gains[layer_id])
        list_one.append(g_one)
        list_two.append(g_two)
        list_gain.append(g_gain)
    acc_one, acc_two, acc_gain = acc_all
    return d_rows, (acc_one + jnp.stack(list_one[::-1]), acc_two + jnp.stack(list_two[::-1]), acc_gain + jnp.stack(list_gain[::-1]))


def keep_bwd(saved_x, d_out, w_one, w_two, gains, acc_all):
    return d_out, acc_all


def solution(mesh):
    n_stage = mesh.shape["stage"]
    n_data = mesh.shape["data"]
    last_stage = n_stage - 1
    east_perm = [(idx_dev, idx_dev + 1) for idx_dev in range(n_stage - 1)]
    west_perm = [(idx_dev + 1, idx_dev) for idx_dev in range(n_stage - 1)]
    mirror_perm = [(idx_dev, n_stage - 1 - idx_dev) for idx_dev in range(n_stage)]

    def local_step(x_in, y_tgt, w_up, w_down, gain):
        n_micro, tokens, width = x_in.shape
        half_micro = n_micro // 2
        depth_local, ff_width = w_up.shape[0], w_up.shape[2]
        tok_total = n_data * n_micro * tokens
        stage_id = lax.axis_index("stage")
        own_w = (w_up, w_down, gain)
        mirror_w = (lax.ppermute(w_up, "stage", mirror_perm), lax.ppermute(w_down, "stage", mirror_perm), lax.ppermute(gain, "stage", mirror_perm))
        x_east = x_in[:half_micro]
        x_west = x_in[half_micro:]
        y_east = y_tgt[:half_micro]
        y_west = y_tgt[half_micro:]

        def fwd_dir(k_micro, recv_rows, stash, top_grad, x_src, y_src, is_first, is_last, weights):
            on_mb = (k_micro >= 0) & (k_micro < half_micro)
            at_mb = jnp.clip(k_micro, 0, half_micro - 1)
            x_rows = jnp.where(is_first, lax.dynamic_index_in_dim(x_src, at_mb, 0, False), recv_rows)
            old_saved = lax.dynamic_index_in_dim(stash, at_mb, 0, False)
            out_rows, saved_new = lax.cond(on_mb, stage_fwd, keep_fwd, x_rows, old_saved, weights[0], weights[1], weights[2])
            stash = lax.dynamic_update_index_in_dim(stash, saved_new, at_mb, 0)
            err_rows = out_rows.astype(jnp.float32) - lax.dynamic_index_in_dim(y_src, at_mb, 0, False).astype(jnp.float32)
            at_end = on_mb & is_last
            top_new = jnp.where(at_end, (err_rows / tok_total).astype(jnp.bfloat16), lax.dynamic_index_in_dim(top_grad, at_mb, 0, False))
            top_grad = lax.dynamic_update_index_in_dim(top_grad, top_new, at_mb, 0)
            loss_add = jnp.where(at_end, jnp.sum(err_rows * err_rows), 0.0)
            return out_rows, stash, top_grad, loss_add

        def fwd_step(state_in, step_t):
            recv_east, recv_west, stash_east, stash_west, top_east, top_west, loss_sum = state_in
            out_east, stash_east, top_east, add_east = fwd_dir(step_t - stage_id, recv_east, stash_east, top_east, x_east, y_east, stage_id == 0, stage_id == last_stage, own_w)
            out_west, stash_west, top_west, add_west = fwd_dir(step_t - (last_stage - stage_id), recv_west, stash_west, top_west, x_west, y_west, stage_id == last_stage, stage_id == 0, mirror_w)
            recv_east = lax.ppermute(out_east, "stage", east_perm)
            recv_west = lax.ppermute(out_west, "stage", west_perm)
            return (recv_east, recv_west, stash_east, stash_west, top_east, top_west, loss_sum + add_east + add_west), None

        zero_rows = jnp.zeros((tokens, width), jnp.bfloat16)
        zero_stash = jnp.zeros((half_micro, depth_local, tokens, width), jnp.bfloat16)
        zero_top = jnp.zeros((half_micro, tokens, width), jnp.bfloat16)
        fwd_init = (zero_rows, zero_rows, zero_stash, zero_stash, zero_top, zero_top, jnp.zeros((), jnp.float32))
        n_steps = half_micro + n_stage - 1
        fwd_state = lax.scan(fwd_step, fwd_init, jnp.arange(n_steps))[0]
        stash_east, stash_west, top_east, top_west, loss_sum = fwd_state[2:]

        def bwd_dir(k_micro, recv_rows, stash, top_grad, is_last, weights, acc_all):
            on_mb = (k_micro >= 0) & (k_micro < half_micro)
            at_mb = jnp.clip(k_micro, 0, half_micro - 1)
            d_rows = jnp.where(is_last, lax.dynamic_index_in_dim(top_grad, at_mb, 0, False), recv_rows)
            saved_x = lax.dynamic_index_in_dim(stash, at_mb, 0, False)
            return lax.cond(on_mb, stage_bwd, keep_bwd, saved_x, d_rows, weights[0], weights[1], weights[2], acc_all)

        def bwd_step(state_in, step_t):
            back_east, back_west, acc_east, acc_west = state_in
            dx_east, acc_east = bwd_dir(step_t - (last_stage - stage_id), back_east, stash_east, top_east, stage_id == last_stage, own_w, acc_east)
            dx_west, acc_west = bwd_dir(step_t - stage_id, back_west, stash_west, top_west, stage_id == 0, mirror_w, acc_west)
            back_east = lax.ppermute(dx_east, "stage", west_perm)
            back_west = lax.ppermute(dx_west, "stage", east_perm)
            return (back_east, back_west, acc_east, acc_west), None

        zero_acc = (jnp.zeros((depth_local, width, ff_width), jnp.float32), jnp.zeros((depth_local, ff_width, width), jnp.float32), jnp.zeros((depth_local, width), jnp.float32))
        bwd_state = lax.scan(bwd_step, (zero_rows, zero_rows, zero_acc, zero_acc), jnp.arange(n_steps))[0]
        acc_east, acc_west = bwd_state[2], bwd_state[3]
        from_mirror = lax.ppermute(acc_west, "stage", mirror_perm)
        stage_sum = jax.tree.map(lambda own_acc, far_acc: own_acc + far_acc, acc_east, from_mirror)
        total_grads = lax.psum(stage_sum, "data")
        loss_all = lax.psum(loss_sum, ("data", "stage")) / (tok_total * width)
        return total_grads[0], total_grads[1], total_grads[2], loss_all.reshape(1)

    return jax.shard_map(local_step, mesh=mesh, in_specs=(P(("part", "data"), None, None), P(("part", "data"), None, None), P("stage", None, None), P("stage", None, None), P("stage", None)), out_specs=(P(("part", "stage"), None, None), P(("part", "stage"), None, None), P(("part", "stage"), None), P("part")), check_vma=False)
```

profile of v0, /device:TPU:0, one launch (start us, length us, event | category | flops | bytes accessed | tf_op | source)
XLA Modules:
  0.0 4639.3 jit_solution(3093112480253457329)
XLA Ops:
  14.1 806.3 %collective-permute-done.4 = f32[1,1536]{1,0:T(1,128)} collective-permute-done((f32[1,1536]{1,0:T(1,128)}, f32[1,1536]{1,0:T(1,128)}, u32[]{:S(2)}, u32[]{:S(2)}) %collective-permute-start.4) | collective-permute-done | bytes 6176 | tf_op jit(solution)/shard_map/ppermute | solution.py:86
  823.5 252.1 %while.48 = (s32[]{:T(128)}, bf16[128,1536]{1,0:T(8,128)(2,1)}, bf16[128,1536]{1,0:T(8,128)(2,1)S(1)}, bf16[1,1,128,1536]{3,2,1,0:T(8,128)(2,1)}, bf16[1,1,128,1...) while((s32[]{:T(128)}, bf16[128,1536]{1,0:T(8,128)(2,1)}, ...), condition=%wide.region_9.10_spmd, body=%wide.region_0.9_spmd.sunk | while | flops 9686482944 | bytes 89694808 | solution.py:119
  824.8 16.7 conditional.8
  825.7 15.0 fusion.23
  852.2 21.4 collective-permute-start
  927.0 18.9 collective-permute-start
  967.4 23.9 collective-permute-done.1
  992.6 29.7 collective-permute-start
  1053.1 15.9 conditional.9
  1054.0 15.0 fusion.68
  1128.8 977.7 %while.49 = (s32[]{:T(128)}, bf16[128,1536]{1,0:T(8,128)(2,1)S(1)}, bf16[128,1536]{1,0:T(8,128)(2,1)}, f32[1,1536,6144]{2,1,0:T(8,128)}, f32[1,6144,1536]{2,1,0:...) while((s32[]{:T(128)}, bf16[128,1536]{1,0:T(8,128)(2,1)S(1)}, ...), condition=%wide.region_21.22_spmd, body=%wide.region_10.21_spmd.sunk | while | flops 24253562880 | bytes 460992320 | solution.py:138
  1133.0 94.4 %conditional.11 = (bf16[128,1536]{1,0:T(8,128)(2,1)}, f32[1,1536,6144]{2,1,0:T(8,128)}, f32[1,6144,1536]{2,1,0:T(8,128)}, f32[1,1536]{1,0:T(1,128)}) conditional(s32[]{:T(128)} %convert_element_type.355, (bf16[128,1536]{1,0:T(8,128)(2,1)}, f32[1,1536,6144]{2,1,0:T(8,128)}, f32[1,6144,1536]{2,1,0:T(8,128)}, f32[1,1536]{1,0:T(1,128)}) %tuple.133, ...), branch_computations={%region_16.16_spmd, %region_17.20_spmd} | conditional | flops 12126584832 | bytes 226956896 | solution.py:127
  1172.0 27.4 bitcast_add_fusion.2
  1199.3 28.0 bitcast_add_fusion.3
  1241.0 95.5 %collective-permute-start.3 = (bf16[128,1536]{1,0:T(8,128)(2,1)}, bf16[128,1536]{1,0:T(8,128)(2,1)}, u32[]{:S(2)}, u32[]{:S(2)}) collective-permute-start(bf16[128,1536]{1,0:T(8,128)(2,1)} %get-tuple-element.984), channel_id=1, source_target_pairs={{0,1},{1,2},{2,3},{3,4},{4,5},{5,6},{6,7},{8,9},{9,10},{10,11},{11... | collective-permute-start | bytes 1179656 | tf_op jit(solution)/shard_map/while/body/eval_jaxpr/ppermute | solution.py:134
  1359.2 93.4 %collective-permute-done.2 = bf16[128,1536]{1,0:T(8,128)(2,1)S(1)} collective-permute-done((bf16[128,1536]{1,0:T(8,128)(2,1)}, bf16[128,1536]{1,0:T(8,128)(2,1)S(1)}, u32[]{:S(2)}, u32[]{:S(2)}) %collective-permute-start.2) | collective-permute-done | bytes 393248 | tf_op jit(solution)/shard_map/while/body/eval_jaxpr/ppermute | solution.py:133
  1478.6 93.0 %collective-permute-start.3 = (bf16[128,1536]{1,0:T(8,128)(2,1)}, bf16[128,1536]{1,0:T(8,128)(2,1)}, u32[]{:S(2)}, u32[]{:S(2)}) collective-permute-start(bf16[128,1536]{1,0:T(8,128)(2,1)} %get-tuple-element.984), channel_id=1, source_target_pairs={{0,1},{1,2},{2,3},{3,4},{4,5},{5,6},{6,7},{8,9},{9,10},{10,11},{11... | collective-permute-start | bytes 1179656 | tf_op jit(solution)/shard_map/while/body/eval_jaxpr/ppermute | solution.py:134
  1594.4 184.0 %collective-permute-done.2 = bf16[128,1536]{1,0:T(8,128)(2,1)S(1)} collective-permute-done((bf16[128,1536]{1,0:T(8,128)(2,1)}, bf16[128,1536]{1,0:T(8,128)(2,1)S(1)}, u32[]{:S(2)}, u32[]{:S(2)}) %collective-permute-start.2) | collective-permute-done | bytes 393248 | tf_op jit(solution)/shard_map/while/body/eval_jaxpr/ppermute | solution.py:133
  1784.0 107.8 %collective-permute-start.3 = (bf16[128,1536]{1,0:T(8,128)(2,1)}, bf16[128,1536]{1,0:T(8,128)(2,1)}, u32[]{:S(2)}, u32[]{:S(2)}) collective-permute-start(bf16[128,1536]{1,0:T(8,128)(2,1)} %get-tuple-element.984), channel_id=1, source_target_pairs={{0,1},{1,2},{2,3},{3,4},{4,5},{5,6},{6,7},{8,9},{9,10},{10,11},{11... | collective-permute-start | bytes 1179656 | tf_op jit(solution)/shard_map/while/body/eval_jaxpr/ppermute | solution.py:134
  1895.4 95.8 %collective-permute-done.2 = bf16[128,1536]{1,0:T(8,128)(2,1)S(1)} collective-permute-done((bf16[128,1536]{1,0:T(8,128)(2,1)}, bf16[128,1536]{1,0:T(8,128)(2,1)S(1)}, u32[]{:S(2)}, u32[]{:S(2)}) %collective-permute-start.2) | collective-permute-done | bytes 393248 | tf_op jit(solution)/shard_map/while/body/eval_jaxpr/ppermute | solution.py:133
  2006.2 96.6 %conditional.10 = (bf16[128,1536]{1,0:T(8,128)(2,1)}, f32[1,1536,6144]{2,1,0:T(8,128)}, f32[1,6144,1536]{2,1,0:T(8,128)}, f32[1,1536]{1,0:T(1,128)}) conditional(s32[]{:T(128)} %convert_element_type.354, (bf16[128,1536]{1,0:T(8,128)(2,1)}, f32[1,1536,6144]{2,1,0:T(8,128)}, f32[1,6144,1536]{2,1,0:T(8,128)}, f32[1,1536]{1,0:T(1,128)}) %tuple.131, ...), branch_computations={%region_11.11_spmd, %region_12.15_spmd} | conditional | flops 12126584832 | bytes 228529792 | solution.py:127
  2027.6 14.7 fusion.125
  2046.6 27.7 bitcast_add_fusion
  2074.4 28.3 bitcast_add_fusion.1
  2109.5 809.9 %collective-permute-done.7 = f32[1,1536,6144]{2,1,0:T(8,128)} collective-permute-done((f32[1,1536,6144]{2,1,0:T(8,128)}, f32[1,1536,6144]{2,1,0:T(8,128)}, u32[]{:S(2)}, u32[]{:S(2)}) %collective-permute-start.7) | collective-permute-done | bytes 37748768 | tf_op jit(solution)/shard_map/ppermute | solution.py:140
  2919.4 37.9 add.141
  2957.3 771.1 %collective-permute-done.8 = f32[1,6144,1536]{2,1,0:T(8,128)} collective-permute-done((f32[1,6144,1536]{2,1,0:T(8,128)}, f32[1,6144,1536]{2,1,0:T(8,128)}, u32[]{:S(2)}, u32[]{:S(2)}) %collective-permute-start.8) | collective-permute-done | bytes 37748768 | tf_op jit(solution)/shard_map/ppermute | solution.py:140
  3728.3 38.1 add.142
  3766.5 72.3 %psum.31 = f32[]{:T(128)} all-reduce(f32[]{:T(128)} %get-tuple-element.552), channel_id=1, replica_groups=mesh['part'=1,'data'=16,'stage'=8] {'data','stage'}, use_global_device_ids=true, to_apply=%region_25.26 | all-reduce | flops 1 | bytes 8 | tf_op jit(solution)/shard_map/psum | solution.py:143
  3839.5 40.6 psum.30
  3880.1 702.3 %all-reduce.3.cloned.1.call-done = (f32[1,1536,6144]{2,1,0:T(8,128)}, f32[1,6144,1536]{2,1,0:T(8,128)}) async-done(((f32[1,1536,6144]{2,1,0:T(8,128)}, f32[1,6144,1536]{2,1,0:T(8,128)}), (f32[1,1536,6144]{2,1,0:T(8,128)}, f32[1,6144,1536]{2,1,0:T(8,128)})) %all-reduce.3.cloned.1.call-update) | async-done | bytes 75497488 | tf_op jit(solution)/shard_map/psum | solution.py:142
  4582.4 28.4 copy.87
  (243 shorter events, 391.2 us)
Async XLA Ops:
  7.2 4575.2 %all-reduce.3.cloned.1.call-start = ((), (), s32[]{:S(2)}) async-start(), calls=%async_computation | async-start | bytes 150994944 | tf_op jit(solution)/shard_map/psum | solution.py:142
  7.2 813.1 %collective-permute-start.5 = (bf16[1,1536,6144]{2,1,0:T(8,128)(2,1)}, bf16[1,1536,6144]{2,1,0:T(8,128)(2,1)}, u32[]{:S(2)}, u32[]{:S(2)}) collective-permute-start(bf16[1,1536,6144]{2,1,0:T(8,128)(2,1)} %param.19), channel_id=1, source_target_pairs={{0,7},{1,6},{2,5},{3,4},{4,3},{5,2},{6,1},{7,0},{8,15},{9,14},{10,... | collective-permute-start | bytes 56623112 | tf_op jit(solution)/shard_map/ppermute | solution.py:86
  9.6 810.7 %collective-permute-start.6 = (bf16[1,6144,1536]{2,1,0:T(8,128)(2,1)}, bf16[1,6144,1536]{2,1,0:T(8,128)(2,1)}, u32[]{:S(2)}, u32[]{:S(2)}) collective-permute-start(bf16[1,6144,1536]{2,1,0:T(8,128)(2,1)} %param.20), channel_id=1, source_target_pairs={{0,7},{1,6},{2,5},{3,4},{4,3},{5,2},{6,1},{7,0},{8,15},{9,14},{10,... | collective-permute-start | bytes 56623112 | tf_op jit(solution)/shard_map/ppermute | solution.py:86
  10.2 810.1 %collective-permute-start.4 = (f32[1,1536]{1,0:T(1,128)}, f32[1,1536]{1,0:T(1,128)}, u32[]{:S(2)}, u32[]{:S(2)}) collective-permute-start(f32[1,1536]{1,0:T(1,128)} %param.21), channel_id=1, source_target_pairs={{0,7},{1,6},{2,5},{3,4},{4,3},{5,2},{6,1},{7,0},{8,15},{9,14},{10,... | collective-permute-start | bytes 18440 | tf_op jit(solution)/shard_map/ppermute | solution.py:86
  841.5 9.4 collective-permute-start
  844.3 6.6 collective-permute-start.1
  852.2 28.7 collective-permute-start
  874.4 6.6 collective-permute-start.1
  882.3 12.8 collective-permute-start
  888.5 18.8 collective-permute-start.1
  908.7 17.0 collective-permute-start
  919.1 6.6 collective-permute-start.1
  927.0 26.2 collective-permute-start
  946.7 6.6 collective-permute-start.1
  954.6 12.8 collective-permute-start
  960.8 30.4 collective-permute-start.1
  992.6 37.1 collective-permute-start
  1023.1 18.3 collective-permute-start.1
  1042.8 32.8 collective-permute-start
  1241.0 99.1 %collective-permute-start.3 = (bf16[128,1536]{1,0:T(8,128)(2,1)}, bf16[128,1536]{1,0:T(8,128)(2,1)}, u32[]{:S(2)}, u32[]{:S(2)}) collective-permute-start(bf16[128,1536]{1,0:T(8,128)(2,1)} %get-tuple-element.984), channel_id=1, source_target_pairs={{0,1},{1,2},{2,3},{3,4},{4,5},{5,6},{6,7},{8,9},{9,10},{10,11},{11... | collective-permute-start | bytes 1179656 | tf_op jit(solution)/shard_map/while/body/eval_jaxpr/ppermute | solution.py:134
  1348.1 11.2 collective-permute-start.3
  1357.9 94.7 %collective-permute-start.2 = (bf16[128,1536]{1,0:T(8,128)(2,1)}, bf16[128,1536]{1,0:T(8,128)(2,1)S(1)}, u32[]{:S(2)}, u32[]{:S(2)}) collective-permute-start(bf16[128,1536]{1,0:T(8,128)(2,1)} %get-tuple-element.982), channel_id=1, source_target_pairs={{1,0},{2,1},{3,2},{4,3},{5,4},{6,5},{7,6},{9,8},{10,9},{11,10},{12... | collective-permute-start | bytes 1179656 | tf_op jit(solution)/shard_map/while/body/eval_jaxpr/ppermute | solution.py:133
  1458.3 12.4 collective-permute-start.3
  1478.6 96.7 %collective-permute-start.3 = (bf16[128,1536]{1,0:T(8,128)(2,1)}, bf16[128,1536]{1,0:T(8,128)(2,1)}, u32[]{:S(2)}, u32[]{:S(2)}) collective-permute-start(bf16[128,1536]{1,0:T(8,128)(2,1)} %get-tuple-element.984), channel_id=1, source_target_pairs={{0,1},{1,2},{2,3},{3,4},{4,5},{5,6},{6,7},{8,9},{9,10},{10,11},{11... | collective-permute-start | bytes 1179656 | tf_op jit(solution)/shard_map/while/body/eval_jaxpr/ppermute | solution.py:134
  1583.2 11.2 collective-permute-start.3
  1593.1 185.3 %collective-permute-start.2 = (bf16[128,1536]{1,0:T(8,128)(2,1)}, bf16[128,1536]{1,0:T(8,128)(2,1)S(1)}, u32[]{:S(2)}, u32[]{:S(2)}) collective-permute-start(bf16[128,1536]{1,0:T(8,128)(2,1)} %get-tuple-element.982), channel_id=1, source_target_pairs={{1,0},{2,1},{3,2},{4,3},{5,4},{6,5},{7,6},{9,8},{10,9},{11,10},{12... | collective-permute-start | bytes 1179656 | tf_op jit(solution)/shard_map/while/body/eval_jaxpr/ppermute | solution.py:133
  1784.0 111.4 %collective-permute-start.3 = (bf16[128,1536]{1,0:T(8,128)(2,1)}, bf16[128,1536]{1,0:T(8,128)(2,1)}, u32[]{:S(2)}, u32[]{:S(2)}) collective-permute-start(bf16[128,1536]{1,0:T(8,128)(2,1)} %get-tuple-element.984), channel_id=1, source_target_pairs={{0,1},{1,2},{2,3},{3,4},{4,5},{5,6},{6,7},{8,9},{9,10},{10,11},{11... | collective-permute-start | bytes 1179656 | tf_op jit(solution)/shard_map/while/body/eval_jaxpr/ppermute | solution.py:134
  1894.1 97.1 %collective-permute-start.2 = (bf16[128,1536]{1,0:T(8,128)(2,1)}, bf16[128,1536]{1,0:T(8,128)(2,1)S(1)}, u32[]{:S(2)}, u32[]{:S(2)}) collective-permute-start(bf16[128,1536]{1,0:T(8,128)(2,1)} %get-tuple-element.982), channel_id=1, source_target_pairs={{1,0},{2,1},{3,2},{4,3},{5,4},{6,5},{7,6},{9,8},{10,9},{11,10},{12... | collective-permute-start | bytes 1179656 | tf_op jit(solution)/shard_map/while/body/eval_jaxpr/ppermute | solution.py:133
  1996.8 107.2 %collective-permute-start.3 = (bf16[128,1536]{1,0:T(8,128)(2,1)}, bf16[128,1536]{1,0:T(8,128)(2,1)}, u32[]{:S(2)}, u32[]{:S(2)}) collective-permute-start(bf16[128,1536]{1,0:T(8,128)(2,1)} %get-tuple-element.984), channel_id=1, source_target_pairs={{0,1},{1,2},{2,3},{3,4},{4,5},{5,6},{6,7},{8,9},{9,10},{10,11},{11... | collective-permute-start | bytes 1179656 | tf_op jit(solution)/shard_map/while/body/eval_jaxpr/ppermute | solution.py:134
  2106.5 812.9 %collective-permute-start.7 = (f32[1,1536,6144]{2,1,0:T(8,128)}, f32[1,1536,6144]{2,1,0:T(8,128)}, u32[]{:S(2)}, u32[]{:S(2)}) collective-permute-start(f32[1,1536,6144]{2,1,0:T(8,128)} %get-tuple-element.547), channel_id=1, source_target_pairs={{0,7},{1,6},{2,5},{3,4},{4,3},{5,2},{6,1},{7,0},{8,15},{9,14},{10,... | collective-permute-start | bytes 113246216 | tf_op jit(solution)/shard_map/ppermute | solution.py:140
  2106.6 1621.8 %collective-permute-start.8 = (f32[1,6144,1536]{2,1,0:T(8,128)}, f32[1,6144,1536]{2,1,0:T(8,128)}, u32[]{:S(2)}, u32[]{:S(2)}) collective-permute-start(f32[1,6144,1536]{2,1,0:T(8,128)} %get-tuple-element.549), channel_id=1, source_target_pairs={{0,7},{1,6},{2,5},{3,4},{4,3},{5,2},{6,1},{7,0},{8,15},{9,14},{10,... | collective-permute-start | bytes 113246216 | tf_op jit(solution)/shard_map/ppermute | solution.py:140
  3766.4 73.1 %collective-permute-start.9 = (f32[1,1536]{1,0:T(1,128)}, f32[1,1536]{1,0:T(1,128)S(1)}, u32[]{:S(2)}, u32[]{:S(2)}) collective-permute-start(f32[1,1536]{1,0:T(1,128)} %get-tuple-element.551), channel_id=1, source_target_pairs={{0,7},{1,6},{2,5},{3,4},{4,3},{5,2},{6,1},{7,0},{8,15},{9,14},{10,... | collective-permute-start | bytes 18440 | tf_op jit(solution)/shard_map/ppermute | solution.py:140
  (14 other events, 219.7 us)
Sparse Core Ops, SparseCore 0:
  3766.5 815.7 all-reduce.2
where the time goes:
time: 4660 us; the launch traced here: 4640 us
  waiting for transfers between devices  3520 us (76%)
  starting transfers between devices  462 us (10%)
  matrix products  209 us (4%)
  local copies, waits for them, and re-layouts  147 us (3%)
  other arithmetic  138 us (3%)
  blocking collectives  113 us (2%)
    ppermute x3, waiting for transfers between devices, local_step(): from_mirror = lax.ppermute(acc_west, 'stage', mirror_perm)  1580 us
    ppermute x1, waiting for transfers between devices, local_step(): lax.ppermute(gain, 'stage', mirror_perm)  806 us
    psum x1, waiting for transfers between devices, local_step(): total_grads = lax.psum(stage_sum, 'data')  702 us
    ppermute x8, waiting for transfers between devices, bwd_step(): back_east = lax.ppermute(dx_east, 'stage', west_perm)  385 us
    ppermute x8, starting transfers between devices, bwd_step(): back_west = lax.ppermute(dx_west, 'stage', east_perm)  331 us
    ppermute x8, starting transfers between devices, fwd_step(): recv_east = lax.ppermute(out_east, 'stage', east_perm)  102 us
  transfers between devices with their start and end apart: 39, of which 15 were waited for; matrix products, arithmetic and copies ran while one was open for 4% of the time, Pallas kernels for 0%

commit v1 on v0

v1 whole, which is shorter than its diff:
```python
import functools
import math

import jax
import jax.numpy as jnp
from jax import lax
from jax.experimental import pallas as pl
from jax.experimental.pallas import tpu as pltpu
from jax.sharding import PartitionSpec as P

EPS = 1e-6
C0 = math.sqrt(2.0 / math.pi)
CUB = 0.044715
f32 = jnp.float32
bf16 = jnp.bfloat16
MESH = pl.DeviceIdType.MESH
ROWS = (((0,), (0,)), ((), ()))
LASTS = (((1,), (1,)), ((), ()))


def gelu_u(a):
    t = jnp.tanh(C0 * (a + CUB * (a * a * a)))
    return a * (0.5 * (1.0 + t))


def gelu_both(a):
    a2 = a * a
    t = jnp.tanh(C0 * (a + CUB * (a2 * a)))
    half = 0.5 * (1.0 + t)
    slope = half + (0.5 * a) * (1.0 - t * t) * (C0 + (3.0 * CUB * C0) * a2)
    return a * half, slope


def inv_rms(x):
    return lax.rsqrt(jnp.mean(x * x, axis=-1, keepdims=True) + EPS)


def chain_call(T, D, FF, ny, nz, n_stage, tok_total, cb, nj):
    cw = FF // nj
    last = n_stage - 1
    h = T // 2
    qr = T // 4
    early = (n_stage * 3) // 8

    def kernel(x_ref, y_ref, g_ref, w1, w2, rg, dhg, wt1, wt2, dg_o, loss_o,
               pbuf, qbuf, a_s, acc, xb, ob, rb, db, dxb, ts1, ts2, lossb, exy, exz, dgacc,
               wsem, tsem1, tsem2, xs, xr, ds, dr_, ls, lr, ags, agr, own, exs, exr):
        data = lax.axis_index("data")
        s = lax.axis_index("stage")
        z = data // ny
        y = lax.rem(data, ny)

        def plane(zz, yy):
            return {"data": lax.rem(zz + nz, nz) * ny + lax.rem(yy + ny, ny)}

        yp, ym = lax.rem(y + 1, ny), lax.rem(y + ny - 1, ny)
        zp, zm = lax.rem(z + 1, nz), lax.rem(z + nz - 1, nz)
        nxt = {"stage": lax.rem(s + 1, n_stage)}
        prv = {"stage": lax.rem(s + n_stage - 1, n_stage)}

        cp = pltpu.make_async_copy(w1, pbuf, wsem.at[0])
        cq = pltpu.make_async_copy(w2, qbuf, wsem.at[1])
        cp.start()
        cq.start()

        bar = pltpu.get_barrier_semaphore()
        for dev in [plane(z, y + k) for k in range(1, ny)] + [plane(z + k, y) for k in range(1, nz)] + [nxt, prv]:
            pl.semaphore_signal(bar, inc=1, device_id=dev, device_id_type=MESH)
        pl.semaphore_wait(bar, ny + nz)

        def rc(src, dst, ssem, rsem, dev):
            return pltpu.make_async_remote_copy(src_ref=src, dst_ref=dst, send_sem=ssem, recv_sem=rsem, device_id=dev, device_id_type=MESH)

        yup, ydn, zup, zdn = plane(z, y + 1), plane(z, y - 1), plane(z + 1, y), plane(z - 1, y)
        r0, r1, r2, r3 = pl.ds(0, h), pl.ds(h, h), pl.ds(0, qr), pl.ds(qr, qr)
        r4, r5 = pl.ds(h, qr), pl.ds(h + qr, qr)

        def ag(t, m, src, dst):
            def c(k, a, b, dev):
                return rc(a, b, ags.at[t, m, k], agr.at[t, m, k], dev)
            me = dst.at[z, y, m]
            s1 = [c(0, src.at[m, r0], me.at[r0], yup), c(1, src.at[m, r0], me.at[r0], ydn),
                  c(2, src.at[m, r1], me.at[r1], zup), c(3, src.at[m, r1], me.at[r1], zdn)]
            fw = [(4, (z, ym, m, r2), yup), (5, (z, yp, m, r3), ydn), (6, (zm, y, m, r4), zup), (7, (zp, y, m, r5), zdn)]
            s2 = [c(k, dst.at[i], dst.at[i], dev) for k, i, dev in fw]
            al = slice(None)
            f3 = [(8, (z, al, m, r0), zup), (9, (z, al, m, r0), zdn), (10, (al, y, m, r1), yup), (11, (al, y, m, r1), ydn)]
            s3 = [c(k, dst.at[i], dst.at[i], dev) for k, i, dev in f3]
            f4 = [(12, (zm, al, m, r2), zup), (13, (zp, al, m, r3), zdn), (14, (al, ym, m, r4), yup), (15, (al, yp, m, r5), ydn)]
            s4 = [c(k, dst.at[i], dst.at[i], dev) for k, i, dev in f4]
            loc = pltpu.make_async_copy(src.at[m], me, own.at[t, m])
            return s1, s2, s3, s4, loc

        def ag_start(t, m, src, dst):
            s1, _, _, _, loc = ag(t, m, src, dst)
            for c in s1:
                c.start()
            loc.start()

        def ag_two(t, m, src, dst):
            s1, s2, _, _, _ = ag(t, m, src, dst)
            for a, b in zip(s1, s2):
                a.wait_recv()
                b.start()

        def ag_three(t, m, src, dst):
            _, s2, s3, _, loc = ag(t, m, src, dst)
            loc.wait()
            for c in s2:
                c.wait_recv()
            for c in s3:
                c.start()

        def ag_four(t, m, src, dst):
            _, _, s3, s4, _ = ag(t, m, src, dst)
            for a, b in zip(s3, s4):
                a.wait_recv()
                b.start()

        def ag_end(t, m, src, dst):
            s1, s2, s3, s4, _ = ag(t, m, src, dst)
            for c in s4:
                c.wait_recv()
            for c in s1 + s2 + s3 + s4:
                c.wait_send()

        def ag_rest(t, src, dst):
            for step in (ag_two, ag_three, ag_four, ag_end):
                step(t, 0, src, dst)
                step(t, 1, src, dst)

        def transposes():
            nb = FF // cb

            def cp1(c, slot):
                return pltpu.make_async_copy(ts1.at[slot], wt1.at[pl.ds(c * cb, cb), :], tsem1.at[slot])

            def cp2(c, slot):
                return pltpu.make_async_copy(ts2.at[slot], wt2.at[:, pl.ds(c * cb, cb)], tsem2.at[slot])

            def body(c, _):
                slot = lax.rem(c, 2)

                @pl.when(c >= 2)
                def _():
                    cp1(c - 2, slot).wait()
                    cp2(c - 2, slot).wait()
                off = pl.multiple_of(c * cb, cb)
                ts1[slot] = pbuf[:, pl.ds(off, cb)].T
                ts2[slot] = qbuf[pl.ds(off, cb), :].T
                cp1(c, slot).start()
                cp2(c, slot).start()
                return 0
            lax.fori_loop(0, nb, body, 0)
            for c in (nb - 2, nb - 1):
                cp1(c, c % 2).wait()
                cp2(c, c % 2).wait()

        gain = g_ref[...]

        def two_dots(first):
            def second(j, u):
                p = jnp.dot(u, qbuf[j * cw:(j + 1) * cw, :], preferred_element_type=f32)
                if j == 0:
                    acc[...] = p
                else:
                    acc[...] += p
            u = first(0)
            for j in range(1, nj):
                un = first(j)
                second(j - 1, u)
                u = un
            second(nj - 1, u)

        @pl.when(s == 0)
        def _():
            xb[...] = x_ref[...]
        lossb[...] = jnp.zeros_like(lossb)
        cp.wait()
        cq.wait()

        @pl.when(s >= early)
        def _():
            transposes()

        def x_send(m):
            return rc(ob.at[m], xb.at[m], xs.at[m], xr.at[m], nxt)

        def fwd(m, _):
            @pl.when(s > 0)
            def _():
                x_send(m).wait_recv()
            x = xb[m].astype(f32)
            r = (x * inv_rms(x) * gain).astype(bf16)
            rb[m] = r
            ag_start(0, m, rb, rg)

            def first(j):
                a = jnp.dot(r, pbuf[:, j * cw:(j + 1) * cw], preferred_element_type=f32)
                a_s[m, :, j * cw:(j + 1) * cw] = a
                return gelu_u(a).astype(bf16)
            two_dots(first)
            ob[m] = (xb[m].astype(f32) + acc[...]).astype(bf16)

            @pl.when(s < last)
            def _():
                x_send(m).start()

            @pl.when(s == last)
            def _():
                e = ob[m].astype(f32) - y_ref[m].astype(f32)
                lossb[...] += jnp.sum(e * e)
                db[m] = (e * (1.0 / tok_total)).astype(bf16)
            return 0
        lax.fori_loop(0, 2, fwd, 0)

        @pl.when(s < early)
        def _():
            transposes()
        bp = pltpu.make_async_copy(wt2, pbuf, wsem.at[0])
        bq = pltpu.make_async_copy(wt1, qbuf, wsem.at[1])
        bp.start()
        bq.start()

        l_send = rc(lossb, lossb, ls, lr, prv)

        @pl.when(s == last)
        def _():
            l_send.start()

        @pl.when(s < n_stage // 2)
        def _():
            ag_rest(0, rb, rg)
        bp.wait()
        bq.wait()

        def d_send(m):
            return rc(dxb.at[m], db.at[m], ds.at[m], dr_.at[m], prv)

        dgacc[...] = jnp.zeros_like(dgacc)

        def bwd(m, _):
            @pl.when(s < last)
            def _():
                d_send(m).wait_recv()
            ag_start(1, m, db, dhg)
            dh = db[m]

            def first(j):
                du = jnp.dot(dh, pbuf[:, j * cw:(j + 1) * cw], preferred_element_type=f32)
                _, slope = gelu_both(a_s[m, :, j * cw:(j + 1) * cw])
                return (du * slope).astype(bf16)
            two_dots(first)
            x = xb[m].astype(f32)
            q = inv_rms(x)
            n = x * q
            dr = acc[...]
            dn = dr * gain
            dx = q * (dn - n * jnp.mean(dn * n, axis=-1, keepdims=True))
            dxb[m] = (db[m].astype(f32) + dx).astype(bf16)

            @pl.when(s > 0)
            def _():
                d_send(m).start()
            dgacc[...] += jnp.sum(dr * n, axis=0, keepdims=True)
            return 0
        lax.fori_loop(0, 2, bwd, 0)

        @pl.when(s < last)
        def _():
            l_send.wait_recv()

            @pl.when(s > 0)
            def _():
                l_send.start()

        exy[y, :, :D] = jnp.broadcast_to(dgacc[...], (8, D))
        exy[y, :, D:] = lossb[...]

        def ex(axis, k):
            buf, i, dev = (exy, y, plane(z, y + k)) if axis == 0 else (exz, z, plane(z + k, y))
            return rc(buf.at[i], buf.at[i], exs.at[axis, k - 1], exr.at[axis, k - 1], dev)
        for k in range(1, ny):
            ex(0, k).start()

        @pl.when(s >= n_stage // 2)
        def _():
            ag_rest(0, rb, rg)
        ag_two(1, 0, db, dhg)
        ag_two(1, 1, db, dhg)
        for k in range(1, ny):
            ex(0, k).wait_recv()
        tot = exy[0]
        for k in range(1, ny):
            tot = tot + exy[k]
        exz[z] = tot
        for k in range(1, nz):
            ex(1, k).start()
        for step in (ag_three, ag_four):
            step(1, 0, db, dhg)
            step(1, 1, db, dhg)
        for k in range(1, nz):
            ex(1, k).wait_recv()
        tot = exz[0]
        for k in range(1, nz):
            tot = tot + exz[k]
        dg_o[...] = tot[0:1, :D]
        loss_o[...] = tot[0:1, D:] * (1.0 / (tok_total * D))
        ag_end(1, 0, db, dhg)
        ag_end(1, 1, db, dhg)
        for axis, n in ((0, ny), (1, nz)):
            for k in range(1, n):
                ex(axis, k).wait_send()

        @pl.when(s < last)
        def _():
            x_send(0).wait_send()
            x_send(1).wait_send()

        @pl.when(s > 0)
        def _():
            d_send(0).wait_send()
            d_send(1).wait_send()
            l_send.wait_send()

    dma = pltpu.SemaphoreType.DMA
    anyspec = pl.BlockSpec(memory_space=pl.ANY)
    vspec = pl.BlockSpec(memory_space=pltpu.VMEM)
    S = jax.ShapeDtypeStruct
    return pl.pallas_call(
        kernel,
        in_specs=[vspec, vspec, vspec, anyspec, anyspec],
        out_specs=[anyspec, anyspec, anyspec, anyspec, vspec, vspec],
        out_shape=[S((nz, ny, 2, T, D), bf16), S((nz, ny, 2, T, D), bf16), S((FF, D), bf16), S((D, FF), bf16),
                   S((1, D), f32), S((1, 128), f32)],
        scratch_shapes=[
            pltpu.VMEM((D, FF), bf16), pltpu.VMEM((FF, D), bf16), pltpu.VMEM((2, T, FF), f32), pltpu.VMEM((T, D), f32),
            pltpu.VMEM((2, T, D), bf16), pltpu.VMEM((2, T, D), bf16), pltpu.VMEM((2, T, D), bf16),
            pltpu.VMEM((2, T, D), bf16), pltpu.VMEM((2, T, D), bf16),
            pltpu.VMEM((2, cb, D), bf16), pltpu.VMEM((2, D, cb), bf16),
            pltpu.VMEM((8, 128), f32), pltpu.VMEM((ny, 8, D + 128), f32), pltpu.VMEM((nz, 8, D + 128), f32),
            pltpu.VMEM((1, D), f32),
            dma((2,)), dma((2,)), dma((2,)), dma((2,)), dma((2,)), dma((2,)), dma((2,)), dma, dma,
            dma((2, 2, 16)), dma((2, 2, 16)), dma((2, 2)), dma((2, 3)), dma((2, 3))],
        compiler_params=pltpu.CompilerParams(collective_id=0, has_side_effects=True, vmem_limit_bytes=60 << 20),
        cost_estimate=pl.CostEstimate(flops=8 * 2 * T * D * FF * 2, bytes_accessed=6 * D * FF * 2, transcendentals=0),
        name="chain",
    )


def grads_call(T, D, FF, nb, tc, nblk, flip):
    nc = T // tc

    def kernel(r_ref, dh_ref, w1_ref, w2_ref, o1_ref, o2_ref, acc1, uda):
        def first(c):
            base = pl.multiple_of(c * tc, tc)
            a = jnp.dot(r_ref[pl.ds(base, tc), :], w1_ref[...], preferred_element_type=f32)
            du = lax.dot_general(dh_ref[pl.ds(base, tc), :], w2_ref[...], LASTS, preferred_element_type=f32)
            u, slope = gelu_both(a)
            slot = lax.rem(c, 2)
            uda[slot, :, :nb] = u.astype(bf16)
            uda[slot, :, nb:] = (du * slope).astype(bf16)

        def second(c, init):
            base = pl.multiple_of(c * tc, tc)
            slot = lax.rem(c, 2)
            p2 = lax.dot_general(uda[slot, :, :nb], dh_ref[pl.ds(base, tc), :], ROWS, preferred_element_type=f32)
            p1 = lax.dot_general(uda[slot, :, nb:], r_ref[pl.ds(base, tc), :], ROWS, preferred_element_type=f32)
            if init:
                o2_ref[...] = p2
                acc1[...] = p1
            else:
                o2_ref[...] += p2
                acc1[...] += p1
        first(0)
        first(1)
        second(0, True)

        def body(c, _):
            first(c)
            second(c - 1, False)
            return 0
        lax.fori_loop(2, nc, body, 0)
        second(nc - 1, False)
        o1_ref[...] = acc1[...] if flip else acc1[...].T

    S = jax.ShapeDtypeStruct
    n1 = nb * nblk
    full = pl.BlockSpec((T, D), lambda i: (0, 0), pipeline_mode=pl.Buffered(1))
    down = pl.BlockSpec((nb, D), lambda i: (i, 0))
    up = pl.BlockSpec((D, nb), lambda i: (0, i))
    return pl.pallas_call(
        kernel,
        grid=(nblk,),
        in_specs=[full, full, up, down],
        out_specs=[down if flip else up, down],
        out_shape=[S((n1, D) if flip else (D, FF), f32), S((n1 if flip else FF, D), f32)],
        scratch_shapes=[pltpu.VMEM((nb, D), f32), pltpu.VMEM((2, tc, 2 * nb), bf16)],
        compiler_params=pltpu.CompilerParams(vmem_limit_bytes=60 << 20),
        cost_estimate=pl.CostEstimate(flops=8 * n1 * T * D, bytes_accessed=4 * T * D + 12 * n1 * D, transcendentals=0),
        name="grads_slice" if flip else "grads_local",
    )


def place_call(D, FF, ns, n_dev):
    base = (FF - ns * n_dev) // ns

    def kernel(g1, g2, u_in, d_in, u_out, d_out):
        u_out[...] = g1[0].T
        d_out[...] = g2[0]

    S = jax.ShapeDtypeStruct
    src = pl.BlockSpec((1, ns, D), lambda i: (i, 0, 0))
    anyspec = pl.BlockSpec(memory_space=pl.ANY)
    return pl.pallas_call(
        kernel,
        grid=(n_dev,),
        in_specs=[src, src, anyspec, anyspec],
        out_specs=[pl.BlockSpec((D, ns), lambda i: (0, base + i)), pl.BlockSpec((ns, D), lambda i: (base + i, 0))],
        out_shape=[S((D, FF), f32), S((FF, D), f32)],
        input_output_aliases={2: 0, 3: 1},
        cost_estimate=pl.CostEstimate(flops=0, bytes_accessed=16 * ns * n_dev * D, transcendentals=0),
        name="place",
    )


def solution(mesh):
    n_stage = mesh.shape["stage"]
    n_data = mesh.shape["data"]
    ny = int(round(n_data ** 0.5))
    nz = n_data // ny
    ns = 128

    def local_step(x_in, y_tgt, w_up, w_down, gain):
        n_micro, T, D = x_in.shape
        FF = w_up.shape[2]
        w1, w2 = w_up[0], w_down[0]
        tok_total = n_data * n_micro * T
        rg, dhg, _, _, dg, loss = chain_call(T, D, FF, ny, nz, n_stage, tok_total, 256, 4)(x_in, y_tgt, gain, w1, w2)
        rg = rg.reshape(tok_total, D)
        dhg = dhg.reshape(tok_total, D)
        n_loc = FF - ns * n_data
        start = n_loc + lax.axis_index("data") * ns
        s1 = lax.dynamic_slice_in_dim(w1, start, ns, 1)
        s2 = lax.dynamic_slice_in_dim(w2, start, ns, 0)
        p1, p2 = grads_call(tok_total, D, FF, ns, 512, 1, True)(rg, dhg, s1, s2)
        g1 = lax.all_gather(p1, "data", axis=0)
        g2 = lax.all_gather(p2, "data", axis=0)
        up, down = grads_call(tok_total, D, FF, 256, 1024, n_loc // 256, False)(rg, dhg, w1, w2)
        up, down = place_call(D, FF, ns, n_data)(g1, g2, up, down)
        return up[None], down[None], dg, loss[0, :1]

    return jax.shard_map(local_step, mesh=mesh, in_specs=(P(("part", "data"), None, None), P(("part", "data"), None, None), P("stage", None, None), P("stage", None, None), P("stage", None)), out_specs=(P(("part", "stage"), None, None), P(("part", "stage"), None, None), P(("part", "stage"), None), P("part")), check_vma=False)
```

time: 4660 us -> 577 us (0.12)
  the two profiles are of different devices: /device:TPU:0 before, /device:TPU:4 now
where the time goes in v1:
time: 577 us; the launch traced here: 576 us
  Pallas kernels  556 us (96%)
  between operations  15.2 us (3%)
    pallas_call x1, Pallas kernels, local_step(): grads_call(tok_total, D, FF, 256, 1024, n_loc // 256, False)  257 us
    pallas_call x1, Pallas kernels, local_step(): chain_call(T, D, FF, ny, nz, n_stage, tok_total, 256, 4)  254 us
    pallas_call x1, Pallas kernels, local_step(): up, down = place_call(D, FF, ns, n_data)(g1, g2, up, down)  23 us
    pallas_call x1, Pallas kernels, local_step(): p1, p2 = grads_call(tok_total, D, FF, ns, 512, 1, True)(rg, dhg, s1, s2)  22 us
  transfers between devices with their start and end apart: 2, of which 0 were waited for; matrix products, arithmetic and copies ran while one was open for 0% of the time, Pallas kernels for 45%

profile of v1, /device:TPU:4, one launch (start us, length us, event | category | flops | bytes accessed | tf_op | source)
XLA Modules:
  0.0 575.9 jit_solution(10905544047427521942)
XLA Ops:
  7.2 0.0 all-gather.5.cloned.1.call-start
  7.2 1.8 dynamic-slice_bitcast_fusion.1.w1_ref
  9.0 1.8 dynamic-slice_bitcast_fusion.w2_ref
  10.8 253.9 %chain.1 = (bf16[4,4,2,128,1536]{4,3,2,1,0:T(8,128)(2,1)}, bf16[4,4,2,128,1536]{4,3,2,1,0:T(8,128)(2,1)}, bf16[6144,1536]{1,0:T(8,128)(2,1)}, bf16[1536,6144]{1,...) custom-call(bf16[2,128,1536]{2,1,0:T(8,128)(2,1)} %x_ref.1, bf16[2,128,1536]{2,1,0:T(8,128)(2,1)} %y_ref.1, ...), custom_call_target="tpu_custom_call" | custom-call | flops 38654705664 | bytes 113246208 | tf_op jit(solution)/shard_map/chain/pallas_call | solution.py:439
  264.7 22.0 %grads_slice.1 = (f32[128,1536]{1,0:T(8,128)}, f32[128,1536]{1,0:T(8,128)}) custom-call(bf16[4096,1536]{1,0:T(8,128)(2,1)} %bitcast.18, bf16[4096,1536]{1,0:T(8,128)(2,1)} %bitcast.20, bf16[1536,128]{1,0:T(8,128)(2,1)} %dynamic-slice_bitcast_fusion.1.w1_ref, bf16[128,1536]{1,0:T(8,128)(2,1)} %dynamic-slice_bitcast_fusion.w2_ref), custom_call_target="tpu_custom_call" | custom-call | flops 6442450944 | bytes 27525120 | tf_op jit(solution)/shard_map/grads_slice/pallas_call | solution.py:446
  286.7 0.0 all-gather.5.cloned.1.call-update
  286.8 0.3 all-gather.7.cloned.1.call-start
  287.0 0.5 all-gather.7.cloned.1.call-update
  287.5 256.8 %grads_local.1 = (f32[1536,6144]{1,0:T(8,128)}, f32[6144,1536]{1,0:T(8,128)}) custom-call(bf16[4096,1536]{1,0:T(8,128)(2,1)} %bitcast.19, bf16[4096,1536]{1,0:T(8,128)(2,1)} %bitcast.21, bf16[1536,6144]{1,0:T(8,128)(2,1)} %bitcast.23, bf16[6144,1536]{1,0:T(8,128)(2,1)} %bitcast.25), custom_call_target="tpu_custom_call" | custom-call | flops 206158430208 | bytes 100663296 | tf_op jit(solution)/shard_map/grads_local/pallas_call | solution.py:449
  544.3 0.0 all-gather.5.cloned.1.call-done
  544.3 0.0 all-gather.7.cloned.1.call-done
  544.3 0.0 copy-start
  544.4 0.0 copy-start.1
  544.4 23.0 %place.1 = (f32[1536,6144]{1,0:T(8,128)}, f32[6144,1536]{1,0:T(8,128)}) custom-call(f32[16,128,1536]{2,1,0:T(8,128)} %bitcast.16, f32[16,128,1536]{2,1,0:T(8,128)} %bitcast.17, f32[1536,6144]{1,0:T(8,128)} %get-tuple-element.18.u_in, f32[6144,1536]{1,0:T(8,128)} %get-tuple-element.19.d_in), custom_call_target="tpu_custom_call", output_to_operand_aliasing={{0}: (2, {}), {1}: (3, {})} | custom-call | bytes 50331648 | tf_op jit(solution)/shard_map/place/pallas_call | solution.py:450
  567.3 0.0 copy-done
  567.3 0.6 copy.15
  567.9 0.0 copy-done.1
Async XLA Ops:
  7.2 537.2 %all-gather.5.cloned.1.call-start = ((), (), s32[]{:S(2)}) async-start(), calls=%async_computation | async-start | bytes 13369344 | tf_op jit(solution)/shard_map/all_gather | solution.py:447
  286.8 257.6 %all-gather.7.cloned.1.call-start = ((), (), s32[]{:S(2)}) async-start(), calls=%async_computation.1 | async-start | bytes 13369344 | tf_op jit(solution)/shard_map/all_gather | solution.py:448
  544.3 23.0 %copy-start = (f32[1,1536]{1,0:T(1,128)S(1)}, f32[1,1536]{1,0:T(1,128)}, u32[]{:S(2)}) copy-start(f32[1,1536]{1,0:T(1,128)} %get-tuple-element.30) | copy-start | bytes 18436
  544.4 23.6 %copy-start.1 = (f32[1,128]{1,0:T(1,128)S(1)}, f32[1,128]{1,0:T(1,128)}, u32[]{:S(2)}) copy-start(f32[1,128]{1,0:T(1,128)} %get-tuple-element.23) | copy-start | bytes 1540
Sparse Core Ops, SparseCore 0:
  286.9 87.8 all-gather.4
  376.9 89.3 all-gather.6

commit v2 on v1

--- a/solution.py
+++ b/solution.py
@@ -348,79 +348,356 @@
     )
 
 
-def grads_call(T, D, FF, nb, tc, nblk, flip):
+class Sweep:
+    def __init__(self, T, D, nb, tc, sub, nblk, off, refs, w1, w2, out_up, out_down, up_off, down_off):
+        self.T, self.D, self.nb, self.tc, self.sub, self.nblk = T, D, nb, tc, sub, nblk
+        self.off, self.up_off, self.down_off = off, up_off, down_off
+        self.nc = T // tc
+        self.w1, self.w2, self.out_up, self.out_down = w1, w2, out_up, out_down
+        self.R, self.DH, self.w1b, self.w2b, self.o1, self.o2, self.uda, self.udb, self.wsem, self.osem = refs
+
+    def wcopy(self, b):
+        sl = lax.rem(b, 2)
+        at = pl.multiple_of(self.off + b * self.nb, self.nb)
+        return (pltpu.make_async_copy(self.w1.at[:, pl.ds(at, self.nb)], self.w1b.at[sl], self.wsem.at[0, sl]),
+                pltpu.make_async_copy(self.w2.at[pl.ds(at, self.nb), :], self.w2b.at[sl], self.wsem.at[1, sl]))
+
+    def ocopy(self, b):
+        sl = lax.rem(b, 2)
+        up = pl.multiple_of(self.up_off + b * self.nb, self.nb)
+        dn = pl.multiple_of(self.down_off + b * self.nb, self.nb)
+        return (pltpu.make_async_copy(self.o1.at[sl], self.out_up.at[:, pl.ds(up, self.nb)], self.osem.at[0, sl]),
+                pltpu.make_async_copy(self.o2.at[sl], self.out_down.at[pl.ds(dn, self.nb), :], self.osem.at[1, sl]))
+
+    def prefetch(self):
+        for x in self.wcopy(0):
+            x.start()
+
+    def pre(self, i):
+        b, c = i // self.nc, lax.rem(i, self.nc)
+
+        @pl.when((c == 0) & (b < self.nblk))
+        def _():
+            for x in self.wcopy(b):
+                x.wait()
+
+            @pl.when(b + 1 < self.nblk)
+            def _():
+                for x in self.wcopy(b + 1):
+                    x.start()
+
+    def mid(self, i):
+        b, c = i // self.nc, lax.rem(i, self.nc)
+
+        @pl.when((c == 0) & (b >= 2))
+        def _():
+            for x in self.ocopy(b - 2):
+                x.wait()
+
+    def post(self, i):
+        b, c = i // self.nc, lax.rem(i, self.nc)
+
+        @pl.when(c == self.nc - 1)
+        def _():
+            for x in self.ocopy(b):
+                x.start()
+
+    def drain(self):
+        for b in (self.nblk - 2, self.nblk - 1):
+            if b >= 0:
+                for x in self.ocopy(b):
+                    x.wait()
+
+    def step(self, i, dst, src):
+        nb, tc, sub, D = self.nb, self.tc, self.sub, self.D
+        c, sl = lax.rem(i, self.nc), lax.rem(i // self.nc, 2)
+        j = i - 1
+        jc, jl = lax.rem(j, self.nc), lax.rem(j // self.nc, 2)
+
+        def first(k):
+            base = pl.multiple_of(c * tc + k * sub, sub)
+            a = jnp.dot(self.R[pl.ds(base, sub), :], self.w1b[sl], preferred_element_type=f32)
+            du = lax.dot_general(self.DH[pl.ds(base, sub), :], self.w2b[sl], LASTS, preferred_element_type=f32)
+            u, slope = gelu_both(a)
+            dst[k * sub:(k + 1) * sub, :nb] = u.astype(bf16)
+            dst[k * sub:(k + 1) * sub, nb:] = (du * slope).astype(bf16)
+
+        def second(q):
+            keep = jc > 0
+            base = pl.multiple_of(jc * tc, tc)
+            n = slice(q * 256, (q + 1) * 256)
+            p2 = lax.dot_general(src[:, :nb], self.DH[pl.ds(base, tc), n], ROWS, preferred_element_type=f32)
+            self.o2[jl, :, n] = jnp.where(keep, self.o2[jl, :, n], 0.0) + p2
+            p1 = lax.dot_general(self.R[pl.ds(base, tc), n], src[:, nb:], ROWS, preferred_element_type=f32)
+            self.o1[jl, n, :] = jnp.where(keep, self.o1[jl, n, :], 0.0) + p1
+        q = 0
+        for k in range(tc // sub):
+            first(k)
+            while src is not None and q < ((k + 1) * (D // 256)) // (tc // sub):
+                second(q)
+                q += 1
+
+    def run(self, loads, between):
+        loads(0)
+        self.pre(0)
+        self.step(0, self.uda, None)
+
+        def one(i, dst, src):
+            between(i)
+
+            @pl.when(i < self.nc)
+            def _():
+                loads(i)
+            self.pre(i)
+            self.mid(i - 1)
+            self.step(i, dst, src)
+            self.post(i - 1)
+
+        def body(ii, _):
+            one(2 * ii + 1, self.udb, self.uda)
+            one(2 * ii + 2, self.uda, self.udb)
+            return 0
+        lax.fori_loop(0, self.nblk * self.nc // 2, body, 0)
+
+
+def sweep_scratch(T, D, nb, tc):
+    dma = pltpu.SemaphoreType.DMA
+    return [pltpu.VMEM((T, D), bf16), pltpu.VMEM((T, D), bf16), pltpu.VMEM((2, D, nb), bf16), pltpu.VMEM((2, nb, D), bf16),
+            pltpu.VMEM((2, D, nb), f32), pltpu.VMEM((2, nb, D), f32), pltpu.VMEM((tc, 2 * nb), bf16),
+            pltpu.VMEM((tc, 2 * nb), bf16), dma((2, 2)), dma((2, 2))]
+
+
+def spread_call(T, D, FF, ny, nz, ns, nb, tc, sub, nblk, when):
     nc = T // tc
-
-    def kernel(r_ref, dh_ref, w1_ref, w2_ref, o1_ref, o2_ref, acc1, uda):
-        def first(c):
+    n_loc = FF - ns * ny * nz
+    h = ns // 2
+
+    def kernel(rg, dhg, w1, w2, wt1, ga, gb, lu, ld, R, DH, w1b, w2b, o1, o2, uda, udb, wsem, osem,
+               s1b, s2b, sa, sb, lsem, ssem, loc, snd, rcv):
+        data = lax.axis_index("data")
+        z = data // ny
+        y = lax.rem(data, ny)
+
+        def plane(zz, yy):
+            return {"data": lax.rem(zz + nz, nz) * ny + lax.rem(yy + ny, ny)}
+
+        yup, ydn, zup, zdn = plane(z, y + 1), plane(z, y - 1), plane(z + 1, y), plane(z - 1, y)
+        yp, ym, y2 = lax.rem(y + 1, ny), lax.rem(y + ny - 1, ny), lax.rem(y + 2, ny)
+        zp, zm, z2 = lax.rem(z + 1, nz), lax.rem(z + nz - 1, nz), lax.rem(z + 2, nz)
+        start = pl.multiple_of(n_loc + data * ns, 16)
+        sw = [pltpu.make_async_copy(wt1.at[pl.ds(start, ns), :], s1b, ssem.at[0]),
+              pltpu.make_async_copy(w2.at[pl.ds(start, ns), :], s2b, ssem.at[1])]
+        for x in sw:
+            x.start()
+
+        def token_copy(c):
+            rows = pl.ds(pl.multiple_of(c * tc, tc), tc)
+            return (pltpu.make_async_copy(rg.at[rows], R.at[rows], lsem.at[0, c]),
+                    pltpu.make_async_copy(dhg.at[rows], DH.at[rows], lsem.at[1, c]))
+        for c in range(nc):
+            for x in token_copy(c):
+                x.start()
+        bar = pltpu.get_barrier_semaphore()
+        for dev in (yup, ydn, zup, zdn):
+            pl.semaphore_signal(bar, inc=1, device_id=dev, device_id_type=MESH)
+        pl.semaphore_wait(bar, 4)
+        sweep = Sweep(T, D, nb, tc, sub, nblk, 0, (R, DH, w1b, w2b, o1, o2, uda, udb, wsem, osem), w1, w2, lu, ld, 0, 0)
+        sweep.prefetch()
+        for x in sw:
+            x.wait()
+
+        def own(c, _):
+            for x in token_copy(c):
+                x.wait()
             base = pl.multiple_of(c * tc, tc)
-            a = jnp.dot(r_ref[pl.ds(base, tc), :], w1_ref[...], preferred_element_type=f32)
-            du = lax.dot_general(dh_ref[pl.ds(base, tc), :], w2_ref[...], LASTS, preferred_element_type=f32)
-            u, slope = gelu_both(a)
-            slot = lax.rem(c, 2)
-            uda[slot, :, :nb] = u.astype(bf16)
-            uda[slot, :, nb:] = (du * slope).astype(bf16)
-
-        def second(c, init):
-            base = pl.multiple_of(c * tc, tc)
-            slot = lax.rem(c, 2)
-            p2 = lax.dot_general(uda[slot, :, :nb], dh_ref[pl.ds(base, tc), :], ROWS, preferred_element_type=f32)
-            p1 = lax.dot_general(uda[slot, :, nb:], r_ref[pl.ds(base, tc), :], ROWS, preferred_element_type=f32)
-            if init:
-                o2_ref[...] = p2
-                acc1[...] = p1
-            else:
-                o2_ref[...] += p2
-                acc1[...] += p1
-        first(0)
-        first(1)
-        second(0, True)
-
-        def body(c, _):
-            first(c)
-            second(c - 1, False)
+            for k in range(tc // sub):
+                at = pl.multiple_of(base + k * sub, sub)
+                a = lax.dot_general(R[pl.ds(at, sub), :], s1b[...], LASTS, preferred_element_type=f32)
+                du = lax.dot_general(DH[pl.ds(at, sub), :], s2b[...], LASTS, preferred_element_type=f32)
+                u, slope = gelu_both(a)
+                uda[k * sub:(k + 1) * sub, :ns] = u.astype(bf16)
+                udb[k * sub:(k + 1) * sub, :ns] = (du * slope).astype(bf16)
+            keep = c > 0
+            for q in range(D // 256):
+                n = slice(q * 256, (q + 1) * 256)
+                p2 = lax.dot_general(uda[:, :ns], DH[pl.ds(base, tc), n], ROWS, preferred_element_type=f32)
+                sb[:, n] = jnp.where(keep, sb[:, n], 0.0) + p2
+                p1 = lax.dot_general(udb[:, :ns], R[pl.ds(base, tc), n], ROWS, preferred_element_type=f32)
+                sa[:, n] = jnp.where(keep, sa[:, n], 0.0) + p1
             return 0
-        lax.fori_loop(2, nc, body, 0)
-        second(nc - 1, False)
-        o1_ref[...] = acc1[...] if flip else acc1[...].T
-
+        lax.fori_loop(0, nc, own, 0)
+
+        h0, h1 = pl.ds(0, h), pl.ds(h, h)
+        al = pl.ds(0, ns)
+
+        def rc(k, src, dst, dev):
+            return pltpu.make_async_remote_copy(src_ref=src, dst_ref=dst, send_sem=snd.at[k], recv_sem=rcv.at[k], device_id=dev, device_id_type=MESH)
+
+        def thru(k, buf, zz, yy, part, dev):
+            return (k, buf.at[zz, yy, part], buf.at[zz, yy, part], dev)
+        mine_a, mine_b = ga.at[z, y], gb.at[z, y]
+        plan = [
+            [(0, sa, mine_a, yup), (1, sa, mine_a, ydn), (2, sb, mine_b, zup), (3, sb, mine_b, zdn),
+             (4, sa, mine_a, zup), (5, sa, mine_a, zdn), (6, sb, mine_b, yup), (7, sb, mine_b, ydn)],
+            [thru(8, ga, z, ym, h0, yup), thru(9, ga, z, yp, h1, ydn), thru(10, gb, zm, y, h0, zup), thru(11, gb, zp, y, h1, zdn),
+             thru(12, ga, z, ym, al, zup), thru(13, ga, z, ym, al, zdn), thru(14, ga, z, yp, al, zup), thru(15, ga, z, yp, al, zdn),
+             thru(16, gb, zm, y, al, yup), thru(17, gb, zm, y, al, ydn), thru(18, gb, zp, y, al, yup), thru(19, gb, zp, y, al, ydn)],
+            [thru(20, ga, zm, y, h0, zup), thru(21, ga, zp, y, h1, zdn), thru(22, gb, z, ym, h0, yup), thru(23, gb, z, yp, h1, ydn)],
+            [thru(24, ga, z, y2, al, zup), thru(25, ga, z, y2, al, zdn), thru(26, gb, z2, y, al, yup), thru(27, gb, z2, y, al, ydn)],
+            [thru(28, ga, zm, ym, h0, zup), thru(29, ga, zp, ym, h1, zdn), thru(30, ga, zm, yp, h0, zup), thru(31, ga, zp, yp, h1, zdn),
+             thru(32, gb, zm, ym, h0, yup), thru(33, gb, zm, yp, h1, ydn), thru(34, gb, zp, ym, h0, yup), thru(35, gb, zp, yp, h1, ydn)],
+            [thru(36, ga, zm, y2, h0, zup), thru(37, ga, zp, y2, h1, zdn), thru(38, gb, z2, ym, h0, yup), thru(39, gb, z2, yp, h1, ydn)],
+        ]
+        flat = {e[0]: e for group in plan for e in group}
+        needs = [[], range(0, 4), range(4, 8), range(8, 12), range(12, 20), range(24, 28)]
+
+        def act(g):
+            for k in needs[g]:
+                rc(*flat[k]).wait_recv()
+            for e in plan[g]:
+                rc(*e).start()
+        act(0)
+        keep_a = pltpu.make_async_copy(sa, mine_a, loc.at[0])
+        keep_b = pltpu.make_async_copy(sb, mine_b, loc.at[1])
+        keep_a.start()
+        keep_b.start()
+
+        def between(i):
+            for g, at in enumerate(when):
+                @pl.when(i == at)
+                def _(g=g):
+                    act(g + 1)
+        sweep.run(lambda c: None, between)
+        for k in list(range(20, 24)) + list(range(28, 40)):
+            rc(*flat[k]).wait_recv()
+        for k in range(40):
+            rc(*flat[k]).wait_send()
+        keep_a.wait()
+        keep_b.wait()
+        sweep.drain()
+
+    dma = pltpu.SemaphoreType.DMA
+    anyspec = pl.BlockSpec(memory_space=pl.ANY)
     S = jax.ShapeDtypeStruct
-    n1 = nb * nblk
-    full = pl.BlockSpec((T, D), lambda i: (0, 0), pipeline_mode=pl.Buffered(1))
-    down = pl.BlockSpec((nb, D), lambda i: (i, 0))
-    up = pl.BlockSpec((D, nb), lambda i: (0, i))
     return pl.pallas_call(
         kernel,
-        grid=(nblk,),
-        in_specs=[full, full, up, down],
-        out_specs=[down if flip else up, down],
-        out_shape=[S((n1, D) if flip else (D, FF), f32), S((n1 if flip else FF, D), f32)],
-        scratch_shapes=[pltpu.VMEM((nb, D), f32), pltpu.VMEM((2, tc, 2 * nb), bf16)],
-        compiler_params=pltpu.CompilerParams(vmem_limit_bytes=60 << 20),
-        cost_estimate=pl.CostEstimate(flops=8 * n1 * T * D, bytes_accessed=4 * T * D + 12 * n1 * D, transcendentals=0),
-        name="grads_slice" if flip else "grads_local",
+        in_specs=[anyspec] * 5,
+        out_specs=[anyspec] * 4,
+        out_shape=[S((nz, ny, ns, D), f32), S((nz, ny, ns, D), f32), S((D, nb * nblk), f32), S((nb * nblk, D), f32)],
+        scratch_shapes=sweep_scratch(T, D, nb, tc) + [
+            pltpu.VMEM((ns, D), bf16), pltpu.VMEM((ns, D), bf16), pltpu.VMEM((ns, D), f32), pltpu.VMEM((ns, D), f32),
+            dma((2, nc)), dma((2,)), dma((2,)), dma((40,)), dma((40,))],
+        compiler_params=pltpu.CompilerParams(collective_id=1, has_side_effects=True, vmem_limit_bytes=62 << 20),
+        cost_estimate=pl.CostEstimate(flops=8 * nb * nblk * T * D, bytes_accessed=4 * T * D + 12 * nb * nblk * D, transcendentals=0),
+        name="spread",
     )
 
 
-def place_call(D, FF, ns, n_dev):
-    base = (FF - ns * n_dev) // ns
-
-    def kernel(g1, g2, u_in, d_in, u_out, d_out):
-        u_out[...] = g1[0].T
-        d_out[...] = g2[0]
-
+def final_call(T, D, FF, n_dev, ns, nb, tc, sub, done):
+    nc = T // tc
+    n_loc = FF - ns * n_dev
+    nblk = n_loc // nb - done
+    n_sp = ns * n_dev
+    turns = nblk * nc
+    rows = 128
+    tasks = done * nb // rows + n_sp // rows
+    per = -(-tasks // turns)
+
+    def kernel(rg, dhg, w1, w2, ga, gb, lu, ld, up, down, R, DH, w1b, w2b, o1, o2, uda, udb, wsem, osem,
+               cu, cd, ct, lsem, isem, tsem):
+        def token_copy(c):
+            r = pl.ds(pl.multiple_of(c * tc, tc), tc)
+            return (pltpu.make_async_copy(rg.at[r], R.at[r], lsem.at[0, c]),
+                    pltpu.make_async_copy(dhg.at[r], DH.at[r], lsem.at[1, c]))
+        sweep = Sweep(T, D, nb, tc, sub, nblk, done * nb, (R, DH, w1b, w2b, o1, o2, uda, udb, wsem, osem), w1, w2, up, down,
+                      done * nb, done * nb)
+        sweep.prefetch()
+        for c in range(nc):
+            for x in token_copy(c):
+                x.start()
+        n_l = done * nb // rows
+
+        def ins(t, k):
+            lo = pl.multiple_of(lax.min(t, n_l - 1) * rows, rows)
+            sp = pl.multiple_of(lax.max(t - n_l, 0) * rows, rows)
+            return ([pltpu.make_async_copy(ld.at[pl.ds(lo, rows), :], cd.at[k], isem.at[0, k]),
+                     pltpu.make_async_copy(lu.at[:, pl.ds(lo, rows)], cu.at[k], isem.at[1, k])],
+                    [pltpu.make_async_copy(gb.at[pl.ds(sp, rows), :], cd.at[k], isem.at[0, k]),
+                     pltpu.make_async_copy(ga.at[pl.ds(sp, rows), :], ct.at[k], isem.at[1, k])])
+
+        def outs(t, k):
+            at = pl.multiple_of(jnp.where(t < n_l, t * rows, n_loc + (t - n_l) * rows), rows)
+            return [pltpu.make_async_copy(cd.at[k], down.at[pl.ds(at, rows), :], tsem.at[0, k]),
+                    pltpu.make_async_copy(cu.at[k], up.at[:, pl.ds(at, rows)], tsem.at[1, k])]
+
+        def each(t, which):
+            @pl.when(t < n_l)
+            def _():
+                for x in ins(t, lax.rem(t, 2 * per))[0]:
+                    getattr(x, which)()
+
+            @pl.when((t >= n_l) & (t < tasks))
+            def _():
+                for x in ins(t, lax.rem(t, 2 * per))[1]:
+                    getattr(x, which)()
+
+        def fetch(g):
+            def one(k, _):
+                each(g * per + k, "start")
+                return 0
+            lax.fori_loop(0, per, one, 0)
+
+        def put(g):
+            def one(k, _):
+                t = g * per + k
+                each(t, "wait")
+                slot = lax.rem(t, 2 * per)
+
+                @pl.when((t >= n_l) & (t < tasks))
+                def _():
+                    cu[slot] = ct[slot].T
+
+                @pl.when(t < tasks)
+                def _():
+                    for x in outs(t, slot):
+                        x.start()
+                return 0
+            lax.fori_loop(0, per, one, 0)
+
+        def settle(g):
+            def one(k, _):
+                t = g * per + k
+
+                @pl.when((t >= 0) & (t < tasks))
+                def _():
+                    for x in outs(t, lax.rem(t, 2 * per)):
+                        x.wait()
+                return 0
+            lax.fori_loop(0, per, one, 0)
+        fetch(0)
+
+        def between(i):
+            settle(i - 2)
+            fetch(i)
+            put(i - 1)
+        sweep.run(lambda c: [x.wait() for x in token_copy(c)], between)
+        settle(turns - 1)
+        sweep.drain()
+
+    dma = pltpu.SemaphoreType.DMA
+    anyspec = pl.BlockSpec(memory_space=pl.ANY)
     S = jax.ShapeDtypeStruct
-    src = pl.BlockSpec((1, ns, D), lambda i: (i, 0, 0))
-    anyspec = pl.BlockSpec(memory_space=pl.ANY)
     return pl.pallas_call(
         kernel,
-        grid=(n_dev,),
-        in_specs=[src, src, anyspec, anyspec],
-        out_specs=[pl.BlockSpec((D, ns), lambda i: (0, base + i)), pl.BlockSpec((ns, D), lambda i: (base + i, 0))],
+        in_specs=[anyspec] * 8,
+        out_specs=[anyspec] * 2,
         out_shape=[S((D, FF), f32), S((FF, D), f32)],
-        input_output_aliases={2: 0, 3: 1},
-        cost_estimate=pl.CostEstimate(flops=0, bytes_accessed=16 * ns * n_dev * D, transcendentals=0),
-        name="place",
+        scratch_shapes=sweep_scratch(T, D, nb, tc) + [
+            pltpu.VMEM((2 * per, D, rows), f32), pltpu.VMEM((2 * per, rows, D), f32), pltpu.VMEM((2 * per, rows, D), f32),
+            dma((2, nc)), dma((2, 2 * per)), dma((2, 2 * per))],
+        compiler_params=pltpu.CompilerParams(vmem_limit_bytes=63 << 20),
+        cost_estimate=pl.CostEstimate(flops=8 * nb * nblk * T * D, bytes_accessed=4 * T * D + 24 * FF * D, transcendentals=0),
+        name="final",
     )
 
 
@@ -429,25 +706,21 @@
     n_data = mesh.shape["data"]
     ny = int(round(n_data ** 0.5))
     nz = n_data // ny
-    ns = 128
+    ns, nb, tc, sub, done = 160, 256, 1024, 256, 11
+    when = (8, 14, 18, 28, 38)
 
     def local_step(x_in, y_tgt, w_up, w_down, gain):
         n_micro, T, D = x_in.shape
         FF = w_up.shape[2]
         w1, w2 = w_up[0], w_down[0]
         tok_total = n_data * n_micro * T
-        rg, dhg, _, _, dg, loss = chain_call(T, D, FF, ny, nz, n_stage, tok_total, 256, 4)(x_in, y_tgt, gain, w1, w2)
+        rg, dhg, wt1, _, dg, loss = chain_call(T, D, FF, ny, nz, n_stage, tok_total, 256, 4)(x_in, y_tgt, gain, w1, w2)
         rg = rg.reshape(tok_total, D)
         dhg = dhg.reshape(tok_total, D)
-        n_loc = FF - ns * n_data
-        start = n_loc + lax.axis_index("data") * ns
-        s1 = lax.dynamic_slice_in_dim(w1, start, ns, 1)
-        s2 = lax.dynamic_slice_in_dim(w2, start, ns, 0)
-        p1, p2 = grads_call(tok_total, D, FF, ns, 512, 1, True)(rg, dhg, s1, s2)
-        g1 = lax.all_gather(p1, "data", axis=0)
-        g2 = lax.all_gather(p2, "data", axis=0)
-        up, down = grads_call(tok_total, D, FF, 256, 1024, n_loc // 256, False)(rg, dhg, w1, w2)
-        up, down = place_call(D, FF, ns, n_data)(g1, g2, up, down)
+        ga, gb, lu, ld = spread_call(tok_total, D, FF, ny, nz, ns, nb, tc, sub, done, when)(rg, dhg, w1, w2, wt1)
+        ga = ga.reshape(ns * n_data, D)
+        gb = gb.reshape(ns * n_data, D)
+        up, down = final_call(tok_total, D, FF, n_data, ns, nb, tc, sub, done)(rg, dhg, w1, w2, ga, gb, lu, ld)
         return up[None], down[None], dg, loss[0, :1]
 
     return jax.shard_map(local_step, mesh=mesh, in_specs=(P(("part", "data"), None, None), P(("part", "data"), None, None), P("stage", None, None), P("stage", None, None), P("stage", None)), out_specs=(P(("part", "stage"), None, None), P(("part", "stage"), None, None), P(("part", "stage"), None), P("part")), check_vma=False)

time: 577 us -> 507 us (0.88)
  Pallas kernels: 556 us -> 504 us
  between operations: 15.2 us -> 1.85 us
    pallas_call x3 -> x2, Pallas kernels: 302 us -> 251 us  [the longest x1 183 us: local_step(): spread_call(tok_total, D, FF, ny, nz, ns, nb, tc, sub, done, when)]
  transfers between devices with their start and end apart: 2 -> 0, of which waited for: 0 -> 0; matrix products, arithmetic and copies ran while one was open for 0% -> 0% of each run, Pallas kernels for 45% -> 0%
where the time goes in v2:
time: 507 us
  Pallas kernels  504 us (99%)
    pallas_call x1, Pallas kernels, local_step(): chain_call(T, D, FF, ny, nz, n_stage, tok_total, 256, 4)  254 us
    pallas_call x1, Pallas kernels, local_step(): spread_call(tok_total, D, FF, ny, nz, ns, nb, tc, sub, done, when)  183 us
    pallas_call x1, Pallas kernels, local_step(): final_call(tok_total, D, FF, n_data, ns, nb, tc, sub, done)  67.9 us

profile of v2, /device:TPU:4, one launch (start us, length us, event | category | flops | bytes accessed | tf_op | source)
XLA Modules:
  0.0 506.9 jit_solution(17622051363883883147)
XLA Ops:
  0.6 253.9 %chain.1 = (bf16[4,4,2,128,1536]{4,3,2,1,0:T(8,128)(2,1)}, bf16[4,4,2,128,1536]{4,3,2,1,0:T(8,128)(2,1)}, bf16[6144,1536]{1,0:T(8,128)(2,1)}, bf16[1536,6144]{1,...) custom-call(bf16[2,128,1536]{2,1,0:T(8,128)(2,1)} %x_ref.1, bf16[2,128,1536]{2,1,0:T(8,128)(2,1)} %y_ref.1, ...), custom_call_target="tpu_custom_call" | custom-call | flops 38654705664 | bytes 113246208 | tf_op jit(solution)/shard_map/chain/pallas_call | solution.py:717
  254.6 182.7 %spread.1 = (f32[4,4,160,1536]{3,2,1,0:T(8,128)}, f32[4,4,160,1536]{3,2,1,0:T(8,128)}, f32[1536,2816]{1,0:T(8,128)}, f32[2816,1536]{1,0:T(8,128)}) custom-call(bf16[4096,1536]{1,0:T(8,128)(2,1)} %bitcast.20, bf16[4096,1536]{1,0:T(8,128)(2,1)} %bitcast.22, bf16[1536,6144]{1,0:T(8,128)(2,1)} %bitcast.11, bf16[6144,1536]{1,0:T(8,128)(2,1)} %bitcast.14, ...), custom_call_target="tpu_custom_call" | custom-call | flops 141733920768 | bytes 77070336 | tf_op jit(solution)/shard_map/spread/pallas_call | solution.py:720
  437.2 0.0 copy-start
  437.2 0.0 copy-start.1
  437.3 67.9 %final.1 = (f32[1536,6144]{1,0:T(8,128)}, f32[6144,1536]{1,0:T(8,128)}) custom-call(bf16[4096,1536]{1,0:T(8,128)(2,1)} %bitcast.21, bf16[4096,1536]{1,0:T(8,128)(2,1)} %bitcast.23, bf16[1536,6144]{1,0:T(8,128)(2,1)} %bitcast.12, bf16[6144,1536]{1,0:T(8,128)(2,1)} %bitcast.15, f32[2560,1536]{1,0:T(8,128)} %bitcast.18, f32[2560,1536]{1,0:T(8,128)} %bitcast.19, ...), custom_call_target="tpu_custom_call" | custom-call | flops 38654705664 | bytes 251658240 | tf_op jit(solution)/shard_map/final/pallas_call | solution.py:723
  505.1 0.0 copy-done
  505.2 0.6 copy.11
  505.8 0.0 copy-done.1
Async XLA Ops:
  437.2 67.9 %copy-start = (f32[1,1536]{1,0:T(1,128)S(1)}, f32[1,1536]{1,0:T(1,128)}, u32[]{:S(2)}) copy-start(f32[1,1536]{1,0:T(1,128)} %get-tuple-element.32) | copy-start | bytes 18436
  437.2 68.5 %copy-start.1 = (f32[1,128]{1,0:T(1,128)S(1)}, f32[1,128]{1,0:T(1,128)}, u32[]{:S(2)}) copy-start(f32[1,128]{1,0:T(1,128)} %get-tuple-element.25) | copy-start | bytes 1540

commit v3 on v2

v3 whole, which is shorter than its diff:
```python
import functools
import math

import jax
import jax.numpy as jnp
from jax import lax
from jax.experimental import pallas as pl
from jax.experimental.pallas import tpu as pltpu
from jax.sharding import PartitionSpec as P

EPS = 1e-6
C0 = math.sqrt(2.0 / math.pi)
CUB = 0.044715
f32 = jnp.float32
bf16 = jnp.bfloat16
MESH = pl.DeviceIdType.MESH
ROWS = (((0,), (0,)), ((), ()))
LASTS = (((1,), (1,)), ((), ()))


def gelu_u(a):
    t = jnp.tanh(C0 * (a + CUB * (a * a * a)))
    return a * (0.5 * (1.0 + t))


def gelu_both(a):
    a2 = a * a
    t = jnp.tanh(C0 * (a + CUB * (a2 * a)))
    half = 0.5 * (1.0 + t)
    slope = half + (0.5 * a) * (1.0 - t * t) * (C0 + (3.0 * CUB * C0) * a2)
    return a * half, slope


def inv_rms(x):
    return lax.rsqrt(jnp.mean(x * x, axis=-1, keepdims=True) + EPS)


NEEDS = ((), (0, 1, 2, 3), (4, 5, 6, 7), (8, 9, 10, 11), (12, 13, 14, 15, 16, 17, 18, 19), (24, 25, 26, 27))
LAST_ONES = tuple(range(20, 24)) + tuple(range(28, 40))


def ring_plan(z, y, nz, ny, mine, at):
    def plane(zz, yy):
        return {"data": lax.rem(zz + nz, nz) * ny + lax.rem(yy + ny, ny)}

    up = (plane(z, y + 1), plane(z + 1, y))
    dn = (plane(z, y - 1), plane(z - 1, y))
    plus = (lambda k: (z, lax.rem(y + k + ny, ny)), lambda k: (lax.rem(z + k + nz, nz), y))

    def cross(p, j, k):
        zz, yy = lax.rem(z + nz + (k if p == 0 else j), nz), lax.rem(y + ny + (j if p == 0 else k), ny)
        return (p, zz, yy)

    groups = []
    groups.append([(2 * p + d, mine(p), at(p, z, y, None), (up, dn)[d][p]) for p in (0, 1) for d in (0, 1)]
                  + [(4 + 2 * p + d, mine(p), at(p, z, y, None), (up, dn)[d][1 - p]) for p in (0, 1) for d in (0, 1)])

    def thru(k, where, half, dev):
        ref = at(*where, half)
        return (k, ref, ref, dev)
    g = [thru(8 + 2 * p + d, cross(p, (-1, 1)[d], 0), d, (up, dn)[d][p]) for p in (0, 1) for d in (0, 1)]
    g += [thru(12 + 4 * p + 2 * j + d, cross(p, (-1, 1)[j], 0), None, (up, dn)[d][1 - p]) for p in (0, 1) for j in (0, 1) for d in (0, 1)]
    groups.append(g)
    groups.append([thru(20 + 2 * p + d, cross(p, 0, (-1, 1)[d]), d, (up, dn)[d][1 - p]) for p in (0, 1) for d in (0, 1)])
    groups.append([thru(24 + 2 * p + d, cross(p, 2, 0), None, (up, dn)[d][1 - p]) for p in (0, 1) for d in (0, 1)])
    groups.append([thru(28 + 4 * p + 2 * j + d, cross(p, (-1, 1)[j], (-1, 1)[d]), d, (up, dn)[d][1 - p])
                   for p in (0, 1) for j in (0, 1) for d in (0, 1)])
    groups.append([thru(36 + 2 * p + d, cross(p, 2, (-1, 1)[d]), d, (up, dn)[d][1 - p]) for p in (0, 1) for d in (0, 1)])
    return groups


def chain_call(T, D, FF, ny, nz, n_stage, tok_total, cb, nj, nb, tc, n_pre, times, ahead):
    cw = FF // nj
    last = n_stage - 1
    h = T // 2
    qr = T // 4
    early = (n_stage * 3) // 8

    nc = tok_total // tc
    n_turn = n_pre // 2 * nc

    def kernel(x_ref, y_ref, g_ref, w1, w2, rg, dhg, wt1, wt2, ap, dg_o, loss_o,
               pbuf, qbuf, a_s, acc, xb, ob, rb, db, dxb, ts1, ts2, ast, lossb, exy, exz, dgacc,
               wsem, tsem1, tsem2, xs, xr, ds, dr_, ls, lr, ags, agr, own, exs, exr, rsem, asem):
        data = lax.axis_index("data")
        s = lax.axis_index("stage")
        z = data // ny
        y = lax.rem(data, ny)

        def plane(zz, yy):
            return {"data": lax.rem(zz + nz, nz) * ny + lax.rem(yy + ny, ny)}

        yp, ym = lax.rem(y + 1, ny), lax.rem(y + ny - 1, ny)
        zp, zm = lax.rem(z + 1, nz), lax.rem(z + nz - 1, nz)
        nxt = {"stage": lax.rem(s + 1, n_stage)}
        prv = {"stage": lax.rem(s + n_stage - 1, n_stage)}

        cp = pltpu.make_async_copy(w1, pbuf, wsem.at[0])
        cq = pltpu.make_async_copy(w2, qbuf, wsem.at[1])
        cp.start()
        cq.start()

        bar = pltpu.get_barrier_semaphore()
        for dev in [plane(z, y + k) for k in range(1, ny)] + [plane(z + k, y) for k in range(1, nz)] + [nxt, prv]:
            pl.semaphore_signal(bar, inc=1, device_id=dev, device_id_type=MESH)
        pl.semaphore_wait(bar, ny + nz)

        def rc(src, dst, ssem, rsem, dev):
            return pltpu.make_async_remote_copy(src_ref=src, dst_ref=dst, send_sem=ssem, recv_sem=rsem, device_id=dev, device_id_type=MESH)

        def ag(t, m, src, dst):
            def at(p, zz, yy, half):
                rows = pl.ds(p * h, h) if half is None else pl.ds(p * h + half * qr, qr)
                return dst.at[zz, yy, m, rows]
            groups = ring_plan(z, y, nz, ny, lambda p: src.at[m, pl.ds(p * h, h)], at)
            entry = {e[0]: e for group in groups for e in group}

            def copy(k):
                _, a, b, dev = entry[k]
                return rc(a, b, ags.at[t, m, k], agr.at[t, m, k], dev)

            def start(g):
                for k in NEEDS[g]:
                    copy(k).wait_recv()
                for e in groups[g]:
                    copy(e[0]).start()
                if g == 0:
                    pltpu.make_async_copy(src.at[m], dst.at[z, y, m], own.at[t, m]).start()

            def finish():
                for k in LAST_ONES:
                    copy(k).wait_recv()
                for k in range(40):
                    copy(k).wait_send()
                pltpu.make_async_copy(src.at[m], dst.at[z, y, m], own.at[t, m]).wait()
            return start, finish

        def ag_start(t, m, src, dst):
            ag(t, m, src, dst)[0](0)

        def ag_half(t, src, dst):
            for g in (1, 2, 3):
                for m in range(2):
                    ag(t, m, src, dst)[0](g)

        def ag_tail(t, src, dst):
            for g in (4, 5):
                for m in range(2):
                    ag(t, m, src, dst)[0](g)
            for m in range(2):
                ag(t, m, src, dst)[1]()

        def transposes():
            nb = FF // cb

            def cp1(c, slot):
                return pltpu.make_async_copy(ts1.at[slot], wt1.at[pl.ds(c * cb, cb), :], tsem1.at[slot])

            def cp2(c, slot):
                return pltpu.make_async_copy(ts2.at[slot], wt2.at[:, pl.ds(c * cb, cb)], tsem2.at[slot])

            def body(c, _):
                slot = lax.rem(c, 2)

                @pl.when(c >= 2)
                def _():
                    cp1(c - 2, slot).wait()
                    cp2(c - 2, slot).wait()
                off = pl.multiple_of(c * cb, cb)
                ts1[slot] = pbuf[:, pl.ds(off, cb)].T
                ts2[slot] = qbuf[pl.ds(off, cb), :].T
                cp1(c, slot).start()
                cp2(c, slot).start()
                return 0
            lax.fori_loop(0, nb, body, 0)
            for c in (nb - 2, nb - 1):
                cp1(c, c % 2).wait()
                cp2(c, c % 2).wait()

        gain = g_ref[...]

        def two_dots(first):
            def second(j, u):
                p = jnp.dot(u, qbuf[j * cw:(j + 1) * cw, :], preferred_element_type=f32)
                if j == 0:
                    acc[...] = p
                else:
                    acc[...] += p
            u = first(0)
            for j in range(1, nj):
                un = first(j)
                second(j - 1, u)
                u = un
            second(nj - 1, u)

        @pl.when(s == 0)
        def _():
            xb[...] = x_ref[...]
        lossb[...] = jnp.zeros_like(lossb)
        cp.wait()
        cq.wait()

        @pl.when(s >= early)
        def _():
            transposes()

        def x_send(m):
            return rc(ob.at[m], xb.at[m], xs.at[m], xr.at[m], nxt)

        def fwd(m, _):
            @pl.when(s > 0)
            def _():
                x_send(m).wait_recv()
            x = xb[m].astype(f32)
            r = (x * inv_rms(x) * gain).astype(bf16)
            rb[m] = r
            ag_start(0, m, rb, rg)

            def first(j):
                a = jnp.dot(r, pbuf[:, j * cw:(j + 1) * cw], preferred_element_type=f32)
                a_s[m, :, j * cw:(j + 1) * cw] = a
                return gelu_u(a).astype(bf16)
            two_dots(first)
            ob[m] = (xb[m].astype(f32) + acc[...]).astype(bf16)

            @pl.when(s < last)
            def _():
                x_send(m).start()

            @pl.when(s == last)
            def _():
                e = ob[m].astype(f32) - y_ref[m].astype(f32)
                lossb[...] += jnp.sum(e * e)
                db[m] = (e * (1.0 / tok_total)).astype(bf16)
            return 0
        lax.fori_loop(0, 2, fwd, 0)

        @pl.when(s < early)
        def _():
            transposes()
        bp = pltpu.make_async_copy(wt2, pbuf, wsem.at[0])
        bq = pltpu.make_async_copy(wt1, qbuf, wsem.at[1])

        @pl.when(s >= n_stage // 2)
        def _():
            bp.start()
            bq.start()

        def r_copy(i):
            dev, m = i // 2, lax.rem(i, 2)
            return pltpu.make_async_copy(rg.at[dev // ny, lax.rem(dev, ny), m], qbuf.at[pl.ds(pl.multiple_of(i * T, T), T), :], rsem.at[i])

        def r_start(i, _):
            r_copy(i).start()
            return 0

        def r_wait(i, _):
            r_copy(i).wait()
            return 0

        def a_copies(i):
            slot, pair = lax.rem(i, 2), i // nc
            rows = pl.ds(pl.multiple_of(lax.rem(i, nc) * tc, tc), tc)
            return [pltpu.make_async_copy(ast.at[slot, k], ap.at[2 * pair + k, rows, :], asem.at[slot, k]) for k in range(2)]

        def turns(lo, hi, tick):
            def turn(i, _):
                tick(i)

                @pl.when(i >= lo + 2)
                def _():
                    for c in a_copies(i - 2):
                        c.wait()
                slot, pair = lax.rem(i, 2), i // nc
                base = pl.multiple_of(lax.rem(i, nc) * tc, tc)
                for k in range(2):
                    cols = pl.ds(pl.multiple_of((2 * pair + k) * nb, nb), nb)
                    ast[slot, k] = jnp.dot(qbuf[pl.ds(base, tc), :], pbuf[:, cols], preferred_element_type=f32)
                for c in a_copies(i):
                    c.start()
                return 0
            lax.fori_loop(lo, hi, turn, 0)

            @pl.when(hi >= lo + 2)
            def _():
                for c in a_copies(hi - 2) + a_copies(hi - 1):
                    c.wait()
        n_early = jnp.where(s == 0, ahead[0], jnp.where(s == 1, ahead[1], jnp.where(s == 2, ahead[2], jnp.where(s == 3, ahead[3], 0))))

        l_send = rc(lossb, lossb, ls, lr, prv)

        @pl.when(s == last)
        def _():
            l_send.start()

        @pl.when(s < last)
        def _():
            ag_half(0, rb, rg)

        @pl.when(s < n_stage // 2)
        def _():
            ag_tail(0, rb, rg)
            lax.fori_loop(0, 2 * ny * nz, r_start, 0)
            lax.fori_loop(0, 2 * ny * nz, r_wait, 0)
            turns(0, n_early, lambda i: None)
            bp.start()
            bq.start()
        bp.wait()
        bq.wait()

        def d_send(m):
            return rc(dxb.at[m], db.at[m], ds.at[m], dr_.at[m], prv)

        dgacc[...] = jnp.zeros_like(dgacc)

        @pl.when(s == 0)
        def _():
            for m in range(2):
                d_send(m).wait_recv()
                ag_start(1, m, db, dhg)
            for m in range(2):
                ag(1, m, db, dhg)[0](1)

        def bwd(m, _):
            @pl.when((s < last) & (s > 0))
            def _():
                d_send(m).wait_recv()

            @pl.when(s > 0)
            def _():
                ag_start(1, m, db, dhg)
            dh = db[m]

            def first(j):
                du = jnp.dot(dh, pbuf[:, j * cw:(j + 1) * cw], preferred_element_type=f32)
                _, slope = gelu_both(a_s[m, :, j * cw:(j + 1) * cw])
                return (du * slope).astype(bf16)
            two_dots(first)
            x = xb[m].astype(f32)
            q = inv_rms(x)
            n = x * q
            dr = acc[...]
            dn = dr * gain
            dx = q * (dn - n * jnp.mean(dn * n, axis=-1, keepdims=True))
            dxb[m] = (db[m].astype(f32) + dx).astype(bf16)

            @pl.when(s > 0)
            def _():
                d_send(m).start()
            dgacc[...] += jnp.sum(dr * n, axis=0, keepdims=True)
            return 0
        lax.fori_loop(0, 2, bwd, 0)

        @pl.when(s < last)
        def _():
            l_send.wait_recv()

            @pl.when(s > 0)
            def _():
                l_send.start()

        exy[y, :, :D] = jnp.broadcast_to(dgacc[...], (8, D))
        exy[y, :, D:] = lossb[...]

        def ex(axis, k):
            buf, i, dev = (exy, y, plane(z, y + k)) if axis == 0 else (exz, z, plane(z + k, y))
            return rc(buf.at[i], buf.at[i], exs.at[axis, k - 1], exr.at[axis, k - 1], dev)
        for k in range(1, ny):
            ex(0, k).start()
        cw1 = pltpu.make_async_copy(w1, pbuf, wsem.at[0])
        cw1.start()

        @pl.when(s == last)
        def _():
            ag_half(0, rb, rg)

        @pl.when(s >= n_stage // 2)
        def _():
            ag_tail(0, rb, rg)

        lax.fori_loop(0, 2 * ny * nz, r_start, 0)
        lax.fori_loop(0, 2 * ny * nz, r_wait, 0)
        cw1.wait()

        def ex_mid():
            for k in range(1, ny):
                ex(0, k).wait_recv()
            tot = exy[0]
            for k in range(1, ny):
                tot = tot + exy[k]
            exz[z] = tot
            for k in range(1, nz):
                ex(1, k).start()

        def ex_last():
            for k in range(1, nz):
                ex(1, k).wait_recv()
            tot = exz[0]
            for k in range(1, nz):
                tot = tot + exz[k]
            dg_o[...] = tot[0:1, :D]
            loss_o[...] = tot[0:1, D:] * (1.0 / (tok_total * D))

        def later(g, m):
            return lambda: ag(1, m, db, dhg)[0](g)
        events = [later(1, 0), later(1, 1), ex_mid, later(2, 0), later(2, 1), later(3, 0), later(3, 1), later(4, 0), later(4, 1),
                  ex_last, later(5, 0), later(5, 1)]
        due = [n_early + jnp.where(s == 0, t0, jnp.where(s == 1, t1, jnp.where(s < n_stage // 2, t2, t3))) for t0, t1, t2, t3 in zip(*times)]

        def tick(i):
            for t, event in zip(due, events):
                @pl.when(i == t)
                def _(event=event):
                    event()
        turns(n_early, n_turn, tick)
        for m in range(2):
            ag(1, m, db, dhg)[1]()
        for axis, n in ((0, ny), (1, nz)):
            for k in range(1, n):
                ex(axis, k).wait_send()

        @pl.when(s < last)
        def _():
            x_send(0).wait_send()
            x_send(1).wait_send()

        @pl.when(s > 0)
        def _():
            d_send(0).wait_send()
            d_send(1).wait_send()
            l_send.wait_send()

    dma = pltpu.SemaphoreType.DMA
    anyspec = pl.BlockSpec(memory_space=pl.ANY)
    vspec = pl.BlockSpec(memory_space=pltpu.VMEM)
    S = jax.ShapeDtypeStruct
    return pl.pallas_call(
        kernel,
        in_specs=[vspec, vspec, vspec, anyspec, anyspec],
        out_specs=[anyspec, anyspec, anyspec, anyspec, anyspec, vspec, vspec],
        out_shape=[S((nz, ny, 2, T, D), bf16), S((nz, ny, 2, T, D), bf16), S((FF, D), bf16), S((D, FF), bf16),
                   S((n_pre, tok_total, nb), f32), S((1, D), f32), S((1, 128), f32)],
        scratch_shapes=[
            pltpu.VMEM((D, FF), bf16), pltpu.VMEM((FF, D), bf16), pltpu.VMEM((2, T, FF), f32), pltpu.VMEM((T, D), f32),
            pltpu.VMEM((2, T, D), bf16), pltpu.VMEM((2, T, D), bf16), pltpu.VMEM((2, T, D), bf16),
            pltpu.VMEM((2, T, D), bf16), pltpu.VMEM((2, T, D), bf16),
            pltpu.VMEM((2, cb, D), bf16), pltpu.VMEM((2, D, cb), bf16), pltpu.VMEM((2, 2, tc, nb), f32),
            pltpu.VMEM((8, 128), f32), pltpu.VMEM((ny, 8, D + 128), f32), pltpu.VMEM((nz, 8, D + 128), f32),
            pltpu.VMEM((1, D), f32),
            dma((2,)), dma((2,)), dma((2,)), dma((2,)), dma((2,)), dma((2,)), dma((2,)), dma, dma,
            dma((2, 2, 40)), dma((2, 2, 40)), dma((2, 2)), dma((2, 3)), dma((2, 3)), dma((2 * ny * nz,)), dma((2, 2))],
        compiler_params=pltpu.CompilerParams(collective_id=0, has_side_effects=True, vmem_limit_bytes=63 << 20),
        cost_estimate=pl.CostEstimate(flops=8 * 2 * T * D * FF * 2, bytes_accessed=6 * D * FF * 2, transcendentals=0),
        name="chain",
    )


class Sweep:
    def __init__(self, T, D, nb, tc, sub, nblk, off, refs, ap, wt2, out_up, out_down, up_off, down_off):
        self.T, self.D, self.nb, self.tc, self.sub, self.nblk = T, D, nb, tc, sub, nblk
        self.off, self.up_off, self.down_off = off, up_off, down_off
        self.nc = T // tc
        self.ap, self.wt2, self.out_up, self.out_down = ap, wt2, out_up, out_down
        self.R, self.DH, self.w2b, self.o1, self.o2, self.uda, self.udb, self.aba, self.abb, self.wsem, self.osem, self.asem = refs

    def wcopy(self, b):
        sl = lax.rem(b, 2)
        at = pl.multiple_of(self.off + b * self.nb, self.nb)
        return (pltpu.make_async_copy(self.wt2.at[:, pl.ds(at, self.nb)], self.w2b.at[sl], self.wsem.at[sl]),)

    def acopy(self, i, buf, slot):
        rows = pl.ds(pl.multiple_of(lax.rem(i, self.nc) * self.tc, self.tc), self.tc)
        return pltpu.make_async_copy(self.ap.at[self.off // self.nb + i // self.nc, rows, :], buf, self.asem.at[slot])

    def ocopy(self, b):
        sl = lax.rem(b, 2)
        up = pl.multiple_of(self.up_off + b * self.nb, self.nb)
        dn = pl.multiple_of(self.down_off + b * self.nb, self.nb)
        return (pltpu.make_async_copy(self.o1.at[sl], self.out_up.at[:, pl.ds(up, self.nb)], self.osem.at[0, sl]),
                pltpu.make_async_copy(self.o2.at[sl], self.out_down.at[pl.ds(dn, self.nb), :], self.osem.at[1, sl]))

    def ocopy(self, b):
        sl = lax.rem(b, 2)
        up = pl.multiple_of(self.up_off + b * self.nb, self.nb)
        dn = pl.multiple_of(self.down_off + b * self.nb, self.nb)
        return (pltpu.make_async_copy(self.o1.at[sl], self.out_up.at[:, pl.ds(up, self.nb)], self.osem.at[0, sl]),
                pltpu.make_async_copy(self.o2.at[sl], self.out_down.at[pl.ds(dn, self.nb), :], self.osem.at[1, sl]))

    def prefetch(self):
        for x in self.wcopy(0):
            x.start()
        self.acopy(0, self.aba, 0).start()

    def step(self, i, dst, src, pre):
        nb, tc, sub, D = self.nb, self.tc, self.sub, self.D
        c, sl = lax.rem(i, self.nc), lax.rem(i // self.nc, 2)
        j = i - 1
        jc, jl = lax.rem(j, self.nc), lax.rem(j // self.nc, 2)

        def first(k):
            base = pl.multiple_of(c * tc + k * sub, sub)
            a = pre[k * sub:(k + 1) * sub, :]
            du = jnp.dot(self.DH[pl.ds(base, sub), :], self.w2b[sl], preferred_element_type=f32)
            u, slope = gelu_both(a)
            dst[k * sub:(k + 1) * sub, :nb] = u.astype(bf16)
            dst[k * sub:(k + 1) * sub, nb:] = (du * slope).astype(bf16)

        def second(q):
            keep = jc > 0
            base = pl.multiple_of(jc * tc, tc)
            n = slice(q * 256, (q + 1) * 256)
            p2 = lax.dot_general(src[:, :nb], self.DH[pl.ds(base, tc), n], ROWS, preferred_element_type=f32)
            self.o2[jl, :, n] = jnp.where(keep, self.o2[jl, :, n], 0.0) + p2
            p1 = lax.dot_general(self.R[pl.ds(base, tc), n], src[:, nb:], ROWS, preferred_element_type=f32)
            self.o1[jl, n, :] = jnp.where(keep, self.o1[jl, n, :], 0.0) + p1
        q = 0
        for k in range(tc // sub):
            first(k)
            while src is not None and q < ((k + 1) * (D // 256)) // (tc // sub):
                second(q)
                q += 1

    def prime(self):
        for x in self.wcopy(0):
            x.start()
        self.acopy(0, self.aba, 0).start()
        self.acopy(1, self.abb, 1).start()

    def run(self, loads, between):
        n, nc = self.nblk * self.nc, self.nc
        if loads is not None:
            loads(0)
        for x in self.wcopy(0):
            x.wait()
        for x in self.wcopy(1):
            x.start()
        self.acopy(0, self.aba, 0).wait()
        self.step(0, self.uda, None, self.aba)

        def body(ii, _):
            i = 2 * ii + 1
            b, odd = i // nc, lax.rem(ii, nc // 2)
            between(ii)
            if loads is not None:
                @pl.when(ii < nc // 2)
                def _():
                    loads(i)

                    @pl.when(i + 1 < nc)
                    def _():
                        loads(i + 1)

            @pl.when(odd == 0)
            def _():
                @pl.when(b >= 1)
                def _():
                    for x in self.ocopy(b - 1):
                        x.start()

                @pl.when(b >= 2)
                def _():
                    for x in self.ocopy(b - 2):
                        x.wait()
            self.acopy(lax.min(i + 1, n - 1), self.aba, 0).start()
            self.acopy(i, self.abb, 1).wait()
            self.step(i, self.udb, self.uda, self.abb)

            @pl.when((odd == nc // 2 - 1) & (b + 1 < self.nblk))
            def _():
                for x in self.wcopy(b + 1):
                    x.wait()

                @pl.when(b + 2 < self.nblk)
                def _():
                    for x in self.wcopy(b + 2):
                        x.start()
            self.acopy(lax.min(i + 2, n - 1), self.abb, 1).start()
            self.acopy(lax.min(i + 1, n - 1), self.aba, 0).wait()
            self.step(i + 1, self.uda, self.udb, self.aba)
            return 0
        lax.fori_loop(0, n // 2, body, 0)
        self.acopy(n - 1, self.abb, 1).wait()
        for x in self.ocopy(self.nblk - 1):
            x.start()

    def drain(self):
        for b in (self.nblk - 2, self.nblk - 1):
            for x in self.ocopy(b):
                x.wait()


def sweep_scratch(T, D, nb, tc):
    dma = pltpu.SemaphoreType.DMA
    return [pltpu.VMEM((T, D), bf16), pltpu.VMEM((T, D), bf16), pltpu.VMEM((2, D, nb), bf16),
            pltpu.VMEM((2, D, nb), f32), pltpu.VMEM((2, nb, D), f32), pltpu.VMEM((tc, 2 * nb), bf16), pltpu.VMEM((tc, 2 * nb), bf16),
            pltpu.VMEM((tc, nb), f32), pltpu.VMEM((tc, nb), f32), dma((2,)), dma((2, 2)), dma((2,))]


def spread_call(T, D, FF, ny, nz, ns, nb, tc, sub, nblk, when):
    nc = T // tc
    n_loc = FF - ns * ny * nz

    def kernel(rg, dhg, ap, w1, wt2, ga, gb, lu, ld, R, DH, w2b, o1, o2, uda, udb, aba, abb, wsem, osem, asem,
               s1b, s2b, sb, sn, us, das, lsem, ssem, loc, snd, rcv):
        data = lax.axis_index("data")
        z = data // ny
        y = lax.rem(data, ny)

        def plane(zz, yy):
            return {"data": lax.rem(zz + nz, nz) * ny + lax.rem(yy + ny, ny)}

        yup, ydn, zup, zdn = plane(z, y + 1), plane(z, y - 1), plane(z + 1, y), plane(z - 1, y)
        start = pl.multiple_of(n_loc + data * ns, ns)
        sw = [pltpu.make_async_copy(w1.at[:, pl.ds(start, ns)], s1b, ssem.at[0]),
              pltpu.make_async_copy(wt2.at[:, pl.ds(start, ns)], s2b, ssem.at[1])]
        for x in sw:
            x.start()

        def token_copy(c):
            rows = pl.ds(pl.multiple_of(c * tc, tc), tc)
            return (pltpu.make_async_copy(rg.at[rows], R.at[rows], lsem.at[0, c]),
                    pltpu.make_async_copy(dhg.at[rows], DH.at[rows], lsem.at[1, c]))
        for c in range(nc):
            for x in token_copy(c):
                x.start()
        bar = pltpu.get_barrier_semaphore()
        for dev in (yup, ydn, zup, zdn):
            pl.semaphore_signal(bar, inc=1, device_id=dev, device_id_type=MESH)
        pl.semaphore_wait(bar, 4)
        sweep = Sweep(T, D, nb, tc, sub, nblk, 0, (R, DH, w2b, o1, o2, uda, udb, aba, abb, wsem, osem, asem), ap, wt2, lu, ld, 0, 0)
        sweep.prime()
        for x in sw:
            x.wait()

        def own(c, _):
            for x in token_copy(c):
                x.wait()
            base = pl.multiple_of(c * tc, tc)
            for k in range(tc // sub):
                at = pl.ds(pl.multiple_of(base + k * sub, sub), sub)
                a = jnp.dot(R[at, :], s1b[...], preferred_element_type=f32)
                du = jnp.dot(DH[at, :], s2b[...], preferred_element_type=f32)
                u, slope = gelu_both(a)
                us[at, :] = u.astype(bf16)
                das[at, :] = (du * slope).astype(bf16)
            return 0

        def at(p, zz, yy, half):
            buf, n = ((ga, D), (gb, ns))[p]
            return buf.at[zz, yy] if half is None else buf.at[zz, yy, pl.ds(half * (n // 2), n // 2), :]
        plan = ring_plan(z, y, nz, ny, lambda p: (sn, sb)[p], at)
        entry = {e[0]: e for group in plan for e in group}

        def copy(k):
            _, a, b, dev = entry[k]
            return pltpu.make_async_remote_copy(src_ref=a, dst_ref=b, send_sem=snd.at[k], recv_sem=rcv.at[k], device_id=dev, device_id_type=MESH)

        def act(g):
            for k in NEEDS[g]:
                copy(k).wait_recv()
            for e in plan[g]:
                copy(e[0]).start()
        keep_a = pltpu.make_async_copy(sn, ga.at[z, y], loc.at[0])
        keep_b = pltpu.make_async_copy(sb, gb.at[z, y], loc.at[1])
        lax.fori_loop(0, nc, own, 0)
        sb[...] = lax.dot_general(us[...], DH[...], ROWS, preferred_element_type=f32)
        for k in (2, 3):
            copy(k).start()
        keep_b.start()
        sn[...] = lax.dot_general(das[...], R[...], ROWS, preferred_element_type=f32).T
        for k in (0, 1, 4, 5, 6, 7):
            copy(k).start()
        keep_a.start()

        def between(ii):
            hit = ii == when[0]
            for t in when[1:]:
                hit = hit | (ii == t)

            @pl.when(hit)
            def _():
                for g, t in enumerate(when):
                    @pl.when(ii == t)
                    def _(g=g):
                        act(g + 1)
        sweep.run(None, between)
        for k in LAST_ONES:
            copy(k).wait_recv()
        for k in range(40):
            copy(k).wait_send()
        keep_a.wait()
        keep_b.wait()
        sweep.drain()

    dma = pltpu.SemaphoreType.DMA
    anyspec = pl.BlockSpec(memory_space=pl.ANY)
    S = jax.ShapeDtypeStruct
    return pl.pallas_call(
        kernel,
        in_specs=[anyspec] * 5,
        out_specs=[anyspec] * 4,
        out_shape=[S((nz, ny, D, ns), f32), S((nz, ny, ns, D), f32), S((D, nb * nblk), f32), S((nb * nblk, D), f32)],
        scratch_shapes=sweep_scratch(T, D, nb, tc) + [
            pltpu.VMEM((D, ns), bf16), pltpu.VMEM((D, ns), bf16), pltpu.VMEM((ns, D), f32), pltpu.VMEM((D, ns), f32),
            pltpu.VMEM((T, ns), bf16), pltpu.VMEM((T, ns), bf16), dma((2, nc)), dma((2,)), dma((2,)), dma((40,)), dma((40,))],
        compiler_params=pltpu.CompilerParams(collective_id=1, has_side_effects=True, vmem_limit_bytes=62 << 20),
        cost_estimate=pl.CostEstimate(flops=8 * nb * nblk * T * D, bytes_accessed=4 * T * D + 12 * nb * nblk * D, transcendentals=0),
        name="spread",
    )


def final_call(T, D, FF, n_dev, ns, nb, tc, sub, done):
    nc = T // tc
    n_loc = FF - ns * n_dev
    nblk = n_loc // nb - done
    n_sp = ns * n_dev
    pairs = nblk * nc // 2
    rows = ns
    tasks = done * nb // rows + n_dev
    per = -(-tasks // pairs)

    def kernel(rg, dhg, ap, wt2, ga, gb, lu, ld, up, down, R, DH, w2b, o1, o2, uda, udb, aba, abb, wsem, osem, asem,
               cu, cd, lsem, isem, tsem):
        def token_copy(c):
            r = pl.ds(pl.multiple_of(c * tc, tc), tc)
            return (pltpu.make_async_copy(rg.at[r], R.at[r], lsem.at[0, c]),
                    pltpu.make_async_copy(dhg.at[r], DH.at[r], lsem.at[1, c]))
        sweep = Sweep(T, D, nb, tc, sub, nblk, done * nb, (R, DH, w2b, o1, o2, uda, udb, aba, abb, wsem, osem, asem), ap, wt2, up, down,
                      done * nb, done * nb)
        sweep.prime()
        for c in range(nc):
            for x in token_copy(c):
                x.start()
        n_l = done * nb // rows

        def ins(t, k):
            lo = pl.multiple_of(lax.min(t, n_l - 1) * rows, rows)
            sp = lax.max(t - n_l, 0)
            return ([pltpu.make_async_copy(ld.at[pl.ds(lo, rows), :], cd.at[k], isem.at[0, k]),
                     pltpu.make_async_copy(lu.at[:, pl.ds(lo, rows)], cu.at[k], isem.at[1, k])],
                    [pltpu.make_async_copy(gb.at[sp], cd.at[k], isem.at[0, k]),
                     pltpu.make_async_copy(ga.at[sp], cu.at[k], isem.at[1, k])])

        def outs(t, k):
            at = pl.multiple_of(jnp.where(t < n_l, t * rows, n_loc + (t - n_l) * rows), rows)
            return [pltpu.make_async_copy(cd.at[k], down.at[pl.ds(at, rows), :], tsem.at[0, k]),
                    pltpu.make_async_copy(cu.at[k], up.at[:, pl.ds(at, rows)], tsem.at[1, k])]

        def loop(g, what):
            def one(k, _):
                t = g * per + k

                @pl.when((t >= 0) & (t < tasks))
                def _():
                    what(t, lax.rem(t + 2 * per, 2 * per))
                return 0
            lax.fori_loop(0, per, one, 0)

        def fetch(t, k):
            @pl.when(t < n_l)
            def _():
                for x in ins(t, k)[0]:
                    x.start(priority=1)

            @pl.when(t >= n_l)
            def _():
                for x in ins(t, k)[1]:
                    x.start(priority=1)

        def put(t, k):
            for x in ins(t, k)[0]:
                x.wait()
            for x in outs(t, k):
                x.start(priority=1)

        def settle(t, k):
            for x in outs(t, k):
                x.wait()

        def between(ii):
            loop(ii - 1, settle)
            loop(ii + 1, fetch)
            loop(ii, put)
        loop(0, fetch)
        sweep.run(lambda c: [x.wait() for x in token_copy(c)], between)
        loop(pairs - 1, settle)
        sweep.drain()

    dma = pltpu.SemaphoreType.DMA
    anyspec = pl.BlockSpec(memory_space=pl.ANY)
    S = jax.ShapeDtypeStruct
    return pl.pallas_call(
        kernel,
        in_specs=[anyspec] * 8,
        out_specs=[anyspec] * 2,
        out_shape=[S((D, FF), f32), S((FF, D), f32)],
        scratch_shapes=sweep_scratch(T, D, nb, tc) + [
            pltpu.VMEM((2 * per, D, rows), f32), pltpu.VMEM((2 * per, rows, D), f32),
            dma((2, nc)), dma((2, 2 * per)), dma((2, 2 * per))],
        compiler_params=pltpu.CompilerParams(vmem_limit_bytes=63 << 20),
        cost_estimate=pl.CostEstimate(flops=8 * nb * nblk * T * D, bytes_accessed=4 * T * D + 24 * FF * D, transcendentals=0),
        name="final",
    )


def solution(mesh):
    n_stage = mesh.shape["stage"]
    n_data = mesh.shape["data"]
    ny = int(round(n_data ** 0.5))
    nz = n_data // ny
    ns, nb, tc, sub, done = 128, 256, 1024, 256, 12
    when = (4, 7, 9, 15, 20)
    times = ((-99, -99, 1, 0, 0, 0, 1, 3, 6, 6, 9, 11), (0, 2, 2, 4, 4, 6, 8, 11, 14, 14, 17, 20), (0, 1, 1, 3, 3, 5, 7, 10, 12, 12, 15, 17), (0, 0, 1, 2, 3, 5, 7, 11, 14, 14, 17, 20))
    ahead = (18, 10, 12, 8)

    def local_step(x_in, y_tgt, w_up, w_down, gain):
        n_micro, T, D = x_in.shape
        FF = w_up.shape[2]
        w1, w2 = w_up[0], w_down[0]
        tok_total = n_data * n_micro * T
        n_pre = (FF - ns * n_data) // nb
        rg, dhg, _, wt2, ap, dg, loss = chain_call(T, D, FF, ny, nz, n_stage, tok_total, 256, 4, nb, tc, n_pre, times, ahead)(x_in, y_tgt, gain, w1, w2)
        rg = rg.reshape(tok_total, D)
        dhg = dhg.reshape(tok_total, D)
        ga, gb, lu, ld = spread_call(tok_total, D, FF, ny, nz, ns, nb, tc, sub, done, when)(rg, dhg, ap, w1, wt2)
        ga = ga.reshape(n_data, D, ns)
        gb = gb.reshape(n_data, ns, D)
        up, down = final_call(tok_total, D, FF, n_data, ns, nb, tc, sub, done)(rg, dhg, ap, wt2, ga, gb, lu, ld)
        return up[None], down[None], dg, loss[0, :1]

    return jax.shard_map(local_step, mesh=mesh, in_specs=(P(("part", "data"), None, None), P(("part", "data"), None, None), P("stage", None, None), P("stage", None, None), P("stage", None)), out_specs=(P(("part", "stage"), None, None), P(("part", "stage"), None, None), P(("part", "stage"), None), P("part")), check_vma=False)
```

time: 507 us -> 464 us (0.915)
  the two profiles are of different devices: /device:TPU:4 before, /device:TPU:0 now
where the time goes in v3:
time: 464 us
  Pallas kernels  462 us (100%)
    pallas_call x1, Pallas kernels, local_step(): chain_call(T, D, FF, ny, nz, n_stage, tok_total, 256, 4, nb, tc, n_pre, t...  239 us
    pallas_call x1, Pallas kernels, local_step(): spread_call(tok_total, D, FF, ny, nz, ns, nb, tc, sub, done, when)  152 us
    pallas_call x1, Pallas kernels, local_step(): final_call(tok_total, D, FF, n_data, ns, nb, tc, sub, done)  70.3 us

profile of v3, /device:TPU:0, one launch (start us, length us, event | category | flops | bytes accessed | tf_op | source)
XLA Modules:
  0.0 464.0 jit_solution(1199548475681753592)
XLA Ops:
  0.6 239.4 %chain.1 = (bf16[4,4,2,128,1536]{4,3,2,1,0:T(8,128)(2,1)}, bf16[4,4,2,128,1536]{4,3,2,1,0:T(8,128)(2,1)}, bf16[6144,1536]{1,0:T(8,128)(2,1)}, bf16[1536,6144]{1,...) custom-call(bf16[2,128,1536]{2,1,0:T(8,128)(2,1)} %x_ref.1, ...), custom_call_target="tpu_custom_call" | custom-call | flops 38654705664 | bytes 113246208 | tf_op jit(solution)/shard_map/chain/pallas_call | solution.py:822
  240.0 151.9 %spread.1 = (f32[4,4,1536,128]{3,2,1,0:T(8,128)}, f32[4,4,128,1536]{3,2,1,0:T(8,128)}, f32[1536,3072]{1,0:T(8,128)}, f32[3072,1536]{1,0:T(8,128)}) custom-call(bf16[4096,1536]{1,0:T(8,128)(2,1)} %bitcast.15, bf16[4096,1536]{1,0:T(8,128)(2,1)} %bitcast.17, f32[16,4096,256]{2,1,0:T(8,128)} %get-tuple-element.18.ap, bf16[1536,6144]{1,0:T(8,128)(2,1)} %bitcast.12, ...), custom_call_target="tpu_custom_call" | custom-call | flops 154618822656 | bytes 81788928 | tf_op jit(solution)/shard_map/spread/pallas_call | solution.py:825
  391.9 0.0 copy-start
  391.9 0.0 copy-start.1
  392.0 70.3 %final.1 = (f32[1536,6144]{1,0:T(8,128)}, f32[6144,1536]{1,0:T(8,128)}) custom-call(bf16[4096,1536]{1,0:T(8,128)(2,1)} %bitcast.16, bf16[4096,1536]{1,0:T(8,128)(2,1)} %bitcast.18, f32[16,4096,256]{2,1,0:T(8,128)} %get-tuple-element.18.ap, bf16[1536,6144]{1,0:T(8,128)(2,1)} %get-tuple-element.19.wt2, f32[16,1536,128]{2,1,0:T(8,128)} %bitcast.19, ...), custom_call_target="tpu_custom_call" | custom-call | flops 51539607552 | bytes 251658240 | tf_op jit(solution)/shard_map/final/pallas_call | solution.py:828
  462.3 0.0 copy-done
  462.3 0.6 copy.11
  462.9 0.0 copy-done.1
Async XLA Ops:
  391.9 70.3 %copy-start = (f32[1,1536]{1,0:T(1,128)S(1)}, f32[1,1536]{1,0:T(1,128)}, u32[]{:S(2)}) copy-start(f32[1,1536]{1,0:T(1,128)} %get-tuple-element.34) | copy-start | bytes 18436
  391.9 70.9 %copy-start.1 = (f32[1,128]{1,0:T(1,128)S(1)}, f32[1,128]{1,0:T(1,128)}, u32[]{:S(2)}) copy-start(f32[1,128]{1,0:T(1,128)} %get-tuple-element.27) | copy-start | bytes 1540

commit v4 on v3

--- a/solution.py
+++ b/solution.py
@@ -95,10 +95,20 @@
         nxt = {"stage": lax.rem(s + 1, n_stage)}
         prv = {"stage": lax.rem(s + n_stage - 1, n_stage)}
 
-        cp = pltpu.make_async_copy(w1, pbuf, wsem.at[0])
-        cq = pltpu.make_async_copy(w2, qbuf, wsem.at[1])
-        cp.start()
-        cq.start()
+        def part(j):
+            return pl.ds(pl.multiple_of(j * cw, cw), cw)
+
+        def weights(src_p, src_q, j):
+            return (pltpu.make_async_copy(src_p.at[:, part(j)], pbuf.at[:, part(j)], wsem.at[0, j]),
+                    pltpu.make_async_copy(src_q.at[part(j), :], qbuf.at[part(j), :], wsem.at[1, j]))
+
+        def each_weight(src_p, src_q, what):
+            def one(j, _):
+                for x in weights(src_p, src_q, j):
+                    getattr(x, what)()
+                return 0
+            lax.fori_loop(0, nj, one, 0)
+        each_weight(w1, w2, "start")
 
         bar = pltpu.get_barrier_semaphore()
         for dev in [plane(z, y + k) for k in range(1, ny)] + [plane(z + k, y) for k in range(1, nz)] + [nxt, prv]:
@@ -179,7 +189,22 @@
 
         gain = g_ref[...]
 
-        def two_dots(first):
+        def two_dots(first, slow, src_p, src_q):
+            @pl.when(slow)
+            def _():
+                def one(j, _):
+                    for x in weights(src_p, src_q, j):
+                        x.wait()
+                    p = jnp.dot(first(j), qbuf[part(j), :], preferred_element_type=f32)
+                    acc[...] = jnp.where(j > 0, acc[...], 0.0) + p
+                    return 0
+                lax.fori_loop(0, nj, one, 0)
+
+            @pl.when(jnp.logical_not(slow))
+            def _():
+                fast_dots(first)
+
+        def fast_dots(first):
             def second(j, u):
                 p = jnp.dot(u, qbuf[j * cw:(j + 1) * cw, :], preferred_element_type=f32)
                 if j == 0:
@@ -197,8 +222,10 @@
         def _():
             xb[...] = x_ref[...]
         lossb[...] = jnp.zeros_like(lossb)
-        cp.wait()
-        cq.wait()
+
+        @pl.when(s > 0)
+        def _():
+            each_weight(w1, w2, "wait")
 
         @pl.when(s >= early)
         def _():
@@ -217,10 +244,10 @@
             ag_start(0, m, rb, rg)
 
             def first(j):
-                a = jnp.dot(r, pbuf[:, j * cw:(j + 1) * cw], preferred_element_type=f32)
-                a_s[m, :, j * cw:(j + 1) * cw] = a
+                a = jnp.dot(rb[m], pbuf[:, part(j)], preferred_element_type=f32)
+                a_s[m, :, part(j)] = a
                 return gelu_u(a).astype(bf16)
-            two_dots(first)
+            two_dots(first, (s == 0) & (m == 0), w1, w2)
             ob[m] = (xb[m].astype(f32) + acc[...]).astype(bf16)
 
             @pl.when(s < last)
@@ -238,13 +265,9 @@
         @pl.when(s < early)
         def _():
             transposes()
-        bp = pltpu.make_async_copy(wt2, pbuf, wsem.at[0])
-        bq = pltpu.make_async_copy(wt1, qbuf, wsem.at[1])
-
         @pl.when(s >= n_stage // 2)
         def _():
-            bp.start()
-            bq.start()
+            each_weight(wt2, wt1, "start")
 
         def r_copy(i):
             dev, m = i // 2, lax.rem(i, 2)
@@ -263,7 +286,7 @@
             rows = pl.ds(pl.multiple_of(lax.rem(i, nc) * tc, tc), tc)
             return [pltpu.make_async_copy(ast.at[slot, k], ap.at[2 * pair + k, rows, :], asem.at[slot, k]) for k in range(2)]
 
-        def turns(lo, hi, tick):
+        def turns(lo, hi, tick, whole):
             def turn(i, _):
                 tick(i)
 
@@ -273,9 +296,16 @@
                         c.wait()
                 slot, pair = lax.rem(i, 2), i // nc
                 base = pl.multiple_of(lax.rem(i, nc) * tc, tc)
-                for k in range(2):
+
+                def block(k, _):
                     cols = pl.ds(pl.multiple_of((2 * pair + k) * nb, nb), nb)
                     ast[slot, k] = jnp.dot(qbuf[pl.ds(base, tc), :], pbuf[:, cols], preferred_element_type=f32)
+                    return 0
+                if whole:
+                    block(0, 0)
+                    block(1, 0)
+                else:
+                    lax.fori_loop(0, 2, block, 0)
                 for c in a_copies(i):
                     c.start()
                 return 0
@@ -302,11 +332,12 @@
             ag_tail(0, rb, rg)
             lax.fori_loop(0, 2 * ny * nz, r_start, 0)
             lax.fori_loop(0, 2 * ny * nz, r_wait, 0)
-            turns(0, n_early, lambda i: None)
-            bp.start()
-            bq.start()
-        bp.wait()
-        bq.wait()
+            turns(0, n_early, lambda i: None, False)
+            each_weight(wt2, wt1, "start")
+
+        @pl.when(s < last)
+        def _():
+            each_weight(wt2, wt1, "wait")
 
         def d_send(m):
             return rc(dxb.at[m], db.at[m], ds.at[m], dr_.at[m], prv)
@@ -329,13 +360,12 @@
             @pl.when(s > 0)
             def _():
                 ag_start(1, m, db, dhg)
-            dh = db[m]
 
             def first(j):
-                du = jnp.dot(dh, pbuf[:, j * cw:(j + 1) * cw], preferred_element_type=f32)
-                _, slope = gelu_both(a_s[m, :, j * cw:(j + 1) * cw])
+                du = jnp.dot(db[m], pbuf[:, part(j)], preferred_element_type=f32)
+                _, slope = gelu_both(a_s[m, :, part(j)])
                 return (du * slope).astype(bf16)
-            two_dots(first)
+            two_dots(first, (s == last) & (m == 0), wt2, wt1)
             x = xb[m].astype(f32)
             q = inv_rms(x)
             n = x * q
@@ -367,7 +397,7 @@
             return rc(buf.at[i], buf.at[i], exs.at[axis, k - 1], exr.at[axis, k - 1], dev)
         for k in range(1, ny):
             ex(0, k).start()
-        cw1 = pltpu.make_async_copy(w1, pbuf, wsem.at[0])
+        cw1 = pltpu.make_async_copy(w1, pbuf, wsem.at[0, 0])
         cw1.start()
 
         @pl.when(s == last)
@@ -412,7 +442,7 @@
                 @pl.when(i == t)
                 def _(event=event):
                     event()
-        turns(n_early, n_turn, tick)
+        turns(n_early, n_turn, tick, True)
         for m in range(2):
             ag(1, m, db, dhg)[1]()
         for axis, n in ((0, ny), (1, nz)):
@@ -447,7 +477,7 @@
             pltpu.VMEM((2, cb, D), bf16), pltpu.VMEM((2, D, cb), bf16), pltpu.VMEM((2, 2, tc, nb), f32),
             pltpu.VMEM((8, 128), f32), pltpu.VMEM((ny, 8, D + 128), f32), pltpu.VMEM((nz, 8, D + 128), f32),
             pltpu.VMEM((1, D), f32),
-            dma((2,)), dma((2,)), dma((2,)), dma((2,)), dma((2,)), dma((2,)), dma((2,)), dma, dma,
+            dma((2, nj)), dma((2,)), dma((2,)), dma((2,)), dma((2,)), dma((2,)), dma((2,)), dma, dma,
             dma((2, 2, 40)), dma((2, 2, 40)), dma((2, 2)), dma((2, 3)), dma((2, 3)), dma((2 * ny * nz,)), dma((2, 2))],
         compiler_params=pltpu.CompilerParams(collective_id=0, has_side_effects=True, vmem_limit_bytes=63 << 20),
         cost_estimate=pl.CostEstimate(flops=8 * 2 * T * D * FF * 2, bytes_accessed=6 * D * FF * 2, transcendentals=0),
@@ -663,11 +693,22 @@
         keep_a = pltpu.make_async_copy(sn, ga.at[z, y], loc.at[0])
         keep_b = pltpu.make_async_copy(sb, gb.at[z, y], loc.at[1])
         lax.fori_loop(0, nc, own, 0)
-        sb[...] = lax.dot_general(us[...], DH[...], ROWS, preferred_element_type=f32)
+        half = D // 3
+
+        def down_half(k, _):
+            at = pl.ds(pl.multiple_of(k * half, half), half)
+            sb[:, at] = lax.dot_general(us[...], DH[:, at], ROWS, preferred_element_type=f32)
+            return 0
+
+        def up_half(k, _):
+            at = pl.ds(pl.multiple_of(k * half, half), half)
+            sn[at, :] = lax.dot_general(das[...], R[:, at], ROWS, preferred_element_type=f32).T
+            return 0
+        lax.fori_loop(0, 3, down_half, 0)
         for k in (2, 3):
             copy(k).start()
         keep_b.start()
-        sn[...] = lax.dot_general(das[...], R[...], ROWS, preferred_element_type=f32).T
+        lax.fori_loop(0, 3, up_half, 0)
         for k in (0, 1, 4, 5, 6, 7):
             copy(k).start()
         keep_a.start()
@@ -810,8 +851,8 @@
     nz = n_data // ny
     ns, nb, tc, sub, done = 128, 256, 1024, 256, 12
     when = (4, 7, 9, 15, 20)
-    times = ((-99, -99, 1, 0, 0, 0, 1, 3, 6, 6, 9, 11), (0, 2, 2, 4, 4, 6, 8, 11, 14, 14, 17, 20), (0, 1, 1, 3, 3, 5, 7, 10, 12, 12, 15, 17), (0, 0, 1, 2, 3, 5, 7, 11, 14, 14, 17, 20))
-    ahead = (18, 10, 12, 8)
+    times = ((-99, -99, 0, 0, 0, 0, 0, 1, 1, 2, 2, 3), (0, 2, 2, 4, 4, 6, 8, 11, 14, 14, 17, 20), (0, 1, 1, 3, 3, 5, 7, 10, 12, 12, 15, 17), (0, 1, 1, 4, 4, 7, 9, 14, 17, 17, 21, 24))
+    ahead = (28, 10, 12, 8)
 
     def local_step(x_in, y_tgt, w_up, w_down, gain):
         n_micro, T, D = x_in.shape

time: 464 us -> 455 us (0.981)
  Pallas kernels: 462 us -> 452 us
    pallas_call x1, Pallas kernels: 239 us -> 229 us  [local_step(): chain_call(T, D, FF, ny, nz, n_stage, tok_total, 256, 4, nb, tc, n_pre, t...]
where the time goes in v4:
time: 455 us
  Pallas kernels  452 us (99%)
    pallas_call x1, Pallas kernels, local_step(): chain_call(T, D, FF, ny, nz, n_stage, tok_total, 256, 4, nb, tc, n_pre, t...  229 us
    pallas_call x1, Pallas kernels, local_step(): spread_call(tok_total, D, FF, ny, nz, ns, nb, tc, sub, done, when)  153 us
    pallas_call x1, Pallas kernels, local_step(): final_call(tok_total, D, FF, n_data, ns, nb, tc, sub, done)  70.3 us

profile of v4, /device:TPU:0, one launch (start us, length us, event | category | flops | bytes accessed | tf_op | source)
XLA Modules:
  0.0 454.9 jit_solution(8334519228841378425)
XLA Ops:
  0.6 229.3 %chain.1 = (bf16[4,4,2,128,1536]{4,3,2,1,0:T(8,128)(2,1)}, bf16[4,4,2,128,1536]{4,3,2,1,0:T(8,128)(2,1)}, bf16[6144,1536]{1,0:T(8,128)(2,1)}, bf16[1536,6144]{1,...) custom-call(bf16[2,128,1536]{2,1,0:T(8,128)(2,1)} %x_ref.1, ...), custom_call_target="tpu_custom_call" | custom-call | flops 38654705664 | bytes 113246208 | tf_op jit(solution)/shard_map/chain/pallas_call | solution.py:863
  229.9 152.9 %spread.1 = (f32[4,4,1536,128]{3,2,1,0:T(8,128)}, f32[4,4,128,1536]{3,2,1,0:T(8,128)}, f32[1536,3072]{1,0:T(8,128)}, f32[3072,1536]{1,0:T(8,128)}) custom-call(bf16[4096,1536]{1,0:T(8,128)(2,1)} %bitcast.15, bf16[4096,1536]{1,0:T(8,128)(2,1)} %bitcast.17, f32[16,4096,256]{2,1,0:T(8,128)} %get-tuple-element.18.ap, bf16[1536,6144]{1,0:T(8,128)(2,1)} %bitcast.12, ...), custom_call_target="tpu_custom_call" | custom-call | flops 154618822656 | bytes 81788928 | tf_op jit(solution)/shard_map/spread/pallas_call | solution.py:866
  382.8 0.0 copy-start
  382.8 0.0 copy-start.1
  382.8 70.3 %final.1 = (f32[1536,6144]{1,0:T(8,128)}, f32[6144,1536]{1,0:T(8,128)}) custom-call(bf16[4096,1536]{1,0:T(8,128)(2,1)} %bitcast.16, bf16[4096,1536]{1,0:T(8,128)(2,1)} %bitcast.18, f32[16,4096,256]{2,1,0:T(8,128)} %get-tuple-element.18.ap, bf16[1536,6144]{1,0:T(8,128)(2,1)} %get-tuple-element.19.wt2, f32[16,1536,128]{2,1,0:T(8,128)} %bitcast.19, ...), custom_call_target="tpu_custom_call" | custom-call | flops 51539607552 | bytes 251658240 | tf_op jit(solution)/shard_map/final/pallas_call | solution.py:869
  453.1 0.0 copy-done
  453.1 0.6 copy.11
  453.7 0.0 copy-done.1
Async XLA Ops:
  382.8 70.3 %copy-start = (f32[1,1536]{1,0:T(1,128)S(1)}, f32[1,1536]{1,0:T(1,128)}, u32[]{:S(2)}) copy-start(f32[1,1536]{1,0:T(1,128)} %get-tuple-element.34) | copy-start | bytes 18436
  382.8 70.9 %copy-start.1 = (f32[1,128]{1,0:T(1,128)S(1)}, f32[1,128]{1,0:T(1,128)}, u32[]{:S(2)}) copy-start(f32[1,128]{1,0:T(1,128)} %get-tuple-element.27) | copy-start | bytes 1540

commit v5 on v4

--- a/solution.py
+++ b/solution.py
@@ -851,8 +851,8 @@
     nz = n_data // ny
     ns, nb, tc, sub, done = 128, 256, 1024, 256, 12
     when = (4, 7, 9, 15, 20)
-    times = ((-99, -99, 0, 0, 0, 0, 0, 1, 1, 2, 2, 3), (0, 2, 2, 4, 4, 6, 8, 11, 14, 14, 17, 20), (0, 1, 1, 3, 3, 5, 7, 10, 12, 12, 15, 17), (0, 1, 1, 4, 4, 7, 9, 14, 17, 17, 21, 24))
-    ahead = (28, 10, 12, 8)
+    times = ((-99, -99, 0, 0, 0, 0, 0, 0, 0, 1, 1, 1), (0, 2, 2, 4, 4, 6, 8, 11, 14, 14, 17, 20), (0, 1, 1, 3, 3, 5, 7, 10, 12, 12, 15, 17), (0, 2, 2, 5, 5, 9, 12, 18, 21, 21, 26, 29))
+    ahead = (30, 10, 12, 8)
 
     def local_step(x_in, y_tgt, w_up, w_down, gain):
         n_micro, T, D = x_in.shape

time: 455 us -> 455 us (level)
  no operation moved by 1% of the time
where the time goes in v5:
time: 455 us
  Pallas kernels  452 us (99%)
    pallas_call x1, Pallas kernels, local_step(): chain_call(T, D, FF, ny, nz, n_stage, tok_total, 256, 4, nb, tc, n_pre, t...  229 us
    pallas_call x1, Pallas kernels, local_step(): spread_call(tok_total, D, FF, ny, nz, ns, nb, tc, sub, done, when)  153 us
    pallas_call x1, Pallas kernels, local_step(): final_call(tok_total, D, FF, n_data, ns, nb, tc, sub, done)  70.3 us

profile of v5, /device:TPU:0, one launch (start us, length us, event | category | flops | bytes accessed | tf_op | source)
XLA Modules:
  0.0 454.9 jit_solution(17521763826971583248)
XLA Ops:
  0.6 229.3 %chain.1 = (bf16[4,4,2,128,1536]{4,3,2,1,0:T(8,128)(2,1)}, bf16[4,4,2,128,1536]{4,3,2,1,0:T(8,128)(2,1)}, bf16[6144,1536]{1,0:T(8,128)(2,1)}, bf16[1536,6144]{1,...) custom-call(bf16[2,128,1536]{2,1,0:T(8,128)(2,1)} %x_ref.1, ...), custom_call_target="tpu_custom_call" | custom-call | flops 38654705664 | bytes 113246208 | tf_op jit(solution)/shard_map/chain/pallas_call | solution.py:863
  229.9 152.9 %spread.1 = (f32[4,4,1536,128]{3,2,1,0:T(8,128)}, f32[4,4,128,1536]{3,2,1,0:T(8,128)}, f32[1536,3072]{1,0:T(8,128)}, f32[3072,1536]{1,0:T(8,128)}) custom-call(bf16[4096,1536]{1,0:T(8,128)(2,1)} %bitcast.15, bf16[4096,1536]{1,0:T(8,128)(2,1)} %bitcast.17, f32[16,4096,256]{2,1,0:T(8,128)} %get-tuple-element.18.ap, bf16[1536,6144]{1,0:T(8,128)(2,1)} %bitcast.12, ...), custom_call_target="tpu_custom_call" | custom-call | flops 154618822656 | bytes 81788928 | tf_op jit(solution)/shard_map/spread/pallas_call | solution.py:866
  382.8 0.0 copy-start
  382.8 0.0 copy-start.1
  382.8 70.3 %final.1 = (f32[1536,6144]{1,0:T(8,128)}, f32[6144,1536]{1,0:T(8,128)}) custom-call(bf16[4096,1536]{1,0:T(8,128)(2,1)} %bitcast.16, bf16[4096,1536]{1,0:T(8,128)(2,1)} %bitcast.18, f32[16,4096,256]{2,1,0:T(8,128)} %get-tuple-element.18.ap, bf16[1536,6144]{1,0:T(8,128)(2,1)} %get-tuple-element.19.wt2, f32[16,1536,128]{2,1,0:T(8,128)} %bitcast.19, ...), custom_call_target="tpu_custom_call" | custom-call | flops 51539607552 | bytes 251658240 | tf_op jit(solution)/shard_map/final/pallas_call | solution.py:869
  453.1 0.0 copy-done
  453.1 0.6 copy.11
  453.7 0.0 copy-done.1
Async XLA Ops:
  382.8 70.3 %copy-start = (f32[1,1536]{1,0:T(1,128)S(1)}, f32[1,1536]{1,0:T(1,128)}, u32[]{:S(2)}) copy-start(f32[1,1536]{1,0:T(1,128)} %get-tuple-element.34) | copy-start | bytes 18436
  382.8 70.9 %copy-start.1 = (f32[1,128]{1,0:T(1,128)S(1)}, f32[1,128]{1,0:T(1,128)}, u32[]{:S(2)}) copy-start(f32[1,128]{1,0:T(1,128)} %get-tuple-element.27) | copy-start | bytes 1540
